TPU v7x, 128 devices: a whole 4x4x4 slice. The times are simulated.
128 devices in a mesh: heads: 1, cp: 128 (over z, y, x, core).
Axes of the slice: x: 4, y: 4, z: 4, core: 2. Of those that a mesh axis runs over, the one named last changes fastest.
Arguments:
- queries: bfloat16 [1, 2048, 56, 128], P(None, 'cp', 'heads')
- key_vecs: bfloat16 [6144, 56, 128], P('cp', 'heads')
- value_vecs: bfloat16 [6144, 56, 128], P('cp', 'heads')
- attn_out: bfloat16 [1, 2048, 56, 128], P(None, 'cp', 'heads')
- log_sum_exp: float32 [1, 2048, 56], P(None, 'cp', 'heads')
- grad_out: bfloat16 [1, 2048, 56, 128], P(None, 'cp', 'heads')
Outputs:
- output 1: bfloat16 [1, 2048, 56, 128], P(None, 'cp', 'heads')
- output 2: float32 [6144, 56, 128], P('cp', 'heads')
- output 3: float32 [6144, 56, 128], P('cp', 'heads')
All inputs are finite; a program needn't handle non-finite values.
Results may differ from a plain program's by a relative error of at most 0.00279.
Values are sent between devices in bfloat16 or wider.
A program may use at most 1 GiB of HBM per device.

v0:
```python
import jax
import jax.numpy as jnp
from jax import lax
from jax.sharding import PartitionSpec as P


def tile_backward(q_tile, do_tile, lse_rows, delta_rows, key_tile, value_tile, q_start, k_start, score_scale):
    q_pos = q_start + jnp.arange(q_tile.shape[0])
    k_pos = k_start + jnp.arange(key_tile.shape[0])
    causal = (q_pos[:, None] >= k_pos[None, :])[None]
    scores = jnp.einsum("qhd,khd->hqk", q_tile, key_tile, preferred_element_type=jnp.float32) * score_scale
    weights = jnp.where(causal, jnp.exp(scores - lse_rows[:, :, None]), 0.0)
    part_v = jnp.einsum("hqk,qhd->khd", weights.astype(jnp.bfloat16), do_tile, preferred_element_type=jnp.float32)
    grad_p = jnp.einsum("qhd,khd->hqk", do_tile, value_tile, preferred_element_type=jnp.float32)
    grad_s = (weights * (grad_p - delta_rows[:, :, None])).astype(jnp.bfloat16)
    part_q = jnp.einsum("hqk,khd->qhd", grad_s, key_tile, preferred_element_type=jnp.float32)
    part_k = jnp.einsum("hqk,qhd->khd", grad_s, q_tile, preferred_element_type=jnp.float32) * score_scale
    return part_q, part_k, part_v


def solution(mesh):
    cp_size = mesh.shape["cp"]
    spec_q = P(None, "cp", "heads", None)
    spec_kv = P("cp", "heads", None)
    spec_lse = P(None, "cp", "heads")

    def per_device(queries, key_vecs, value_vecs, attn_out, log_sum_exp, grad_out):
        n_seg, q_local = queries.shape[:2]
        head_dim = queries.shape[3]
        key_local = key_vecs.shape[0]
        seg_len = q_local * cp_size
        prefix0 = key_local * cp_size - n_seg * seg_len
        score_scale = head_dim ** -0.5
        key_start = lax.axis_index("cp") * key_local
        source_offsets = q_local * jnp.arange(cp_size)
        row_delta = jnp.einsum("sqhd,sqhd->sqh", grad_out, attn_out, preferred_element_type=jnp.float32)

        def source_step(acc_pair, tile_in):
            acc_k, acc_v = acc_pair
            q_tile, do_tile, lse_tile, delta_tile, q_start = tile_in
            part_q, part_k, part_v = tile_backward(q_tile, do_tile, lse_tile.T, delta_tile.T, key_vecs, value_vecs, q_start, key_start, score_scale)
            return (acc_k + part_k, acc_v + part_v), part_q

        kv_acc = (jnp.zeros(key_vecs.shape, jnp.float32), jnp.zeros(value_vecs.shape, jnp.float32))
        dq_list = []
        for seg_idx in reversed(range(n_seg)):
            q_all = lax.all_gather(queries[seg_idx], "cp")
            do_all = lax.all_gather(grad_out[seg_idx], "cp")
            lse_all = lax.all_gather(log_sum_exp[seg_idx], "cp")
            delta_all = lax.all_gather(row_delta[seg_idx], "cp")
            q_starts = prefix0 + seg_idx * seg_len + source_offsets
            kv_acc, parts_q = lax.scan(source_step, kv_acc, (q_all, do_all, lse_all, delta_all, q_starts))
            dq_seg = lax.psum_scatter(parts_q, "cp", scatter_dimension=0) * score_scale
            dq_list.append(dq_seg.astype(jnp.bfloat16))
        return jnp.stack(dq_list[::-1]), kv_acc[0], kv_acc[1]

    return jax.shard_map(per_device, mesh=mesh, in_specs=(spec_q, spec_kv, spec_kv, spec_q, spec_lse, spec_q), out_specs=(spec_q, spec_kv, spec_kv), check_vma=False)
```

profile of v0, /device:TPU:0, one launch (start us, length us, event | category | flops | bytes accessed | tf_op | source)
XLA Modules:
  0.0 1825.5 jit_solution(8862258349794343866)
XLA Ops:
  8.7 1.3 copy.27
  11.0 1.2 fusion.9
  12.2 39.0 %all-gather = f32[2048,56]{1,0:T(8,128)} all-gather(f32[16,56]{1,0:T(8,128)S(1)} %fusion.9), channel_id=2, replica_groups=mesh['heads'=1,'cp'=128] {'cp'}, dimensions={0}, use_global_device_ids=true | all-gather | bytes 462336 | tf_op jit(solution)/shard_map/all_gather | solution.py:50
  51.2 35.4 %all_gather.13 = f32[128,16,56]{2,1,0:T(8,128)} all-gather(f32[1,16,56]{2,1,0:T(8,128)S(1)} %copy-done.2), channel_id=1, replica_groups=mesh['heads'=1,'cp'=128] {'cp'}, dimensions={0}, use_global_device_ids=true | all-gather | bytes 462336 | tf_op jit(solution)/shard_map/all_gather | solution.py:49
  86.7 28.7 %all-gather.4.cloned.1.call-done = bf16[128,16,56,128]{3,2,1,0:T(8,128)(2,1)} async-done(((bf16[1,16,56,128]{3,2,1,0:T(8,128)(2,1)}), bf16[128,16,56,128]{3,2,1,0:T(8,128)(2,1)}) %all-gather.4.cloned.1.call-update) | async-done | bytes 29360144 | tf_op jit(solution)/shard_map/all_gather | solution.py:47
  115.3 101.8 %all-gather.6.cloned.1.call-done = bf16[128,16,56,128]{3,2,1,0:T(8,128)(2,1)} async-done(((bf16[1,16,56,128]{3,2,1,0:T(8,128)(2,1)}), bf16[128,16,56,128]{3,2,1,0:T(8,128)(2,1)}) %all-gather.6.cloned.1.call-update) | async-done | bytes 29360144 | tf_op jit(solution)/shard_map/all_gather | solution.py:48
  217.1 860.2 %while.15 = (s32[]{:T(128)}, f32[48,56,128]{2,0,1:T(8,128)S(1)}, f32[48,56,128]{2,0,1:T(8,128)S(1)}, f32[128,16,56,128]{3,2,1,0:T(8,128)}, bf16[128,16,56,128]{3...) while((s32[]{:T(128)}, f32[48,56,128]{2,0,1:T(8,128)S(1)}, ...), condition=%wide.region_1.2_spmd.clone, body=%wide.region_0.1_spmd.clone.sunk | while | flops 57072448 | bytes 14345428 | solution.py:52
  219.4 1.2 constant_dynamic-slice_fusion.7
  226.2 1.2 constant_dynamic-slice_fusion.7
  232.9 1.2 constant_dynamic-slice_fusion.7
  239.6 1.2 constant_dynamic-slice_fusion.7
  246.3 1.2 constant_dynamic-slice_fusion.7
  253.0 1.2 constant_dynamic-slice_fusion.7
  259.8 1.2 constant_dynamic-slice_fusion.7
  266.5 1.2 constant_dynamic-slice_fusion.7
  273.2 1.2 constant_dynamic-slice_fusion.7
  279.9 1.2 constant_dynamic-slice_fusion.7
  286.6 1.2 constant_dynamic-slice_fusion.7
  293.4 1.2 constant_dynamic-slice_fusion.7
  300.1 1.2 constant_dynamic-slice_fusion.7
  306.8 1.2 constant_dynamic-slice_fusion.7
  313.5 1.2 constant_dynamic-slice_fusion.7
  320.2 1.2 constant_dynamic-slice_fusion.7
  327.0 1.2 constant_dynamic-slice_fusion.7
  333.7 1.2 constant_dynamic-slice_fusion.7
  340.4 1.2 constant_dynamic-slice_fusion.7
  347.2 1.2 constant_dynamic-slice_fusion.7
  353.9 1.2 constant_dynamic-slice_fusion.7
  360.7 1.2 constant_dynamic-slice_fusion.7
  367.4 1.2 constant_dynamic-slice_fusion.7
  374.1 1.2 constant_dynamic-slice_fusion.7
  380.8 1.2 constant_dynamic-slice_fusion.7
  387.6 1.2 constant_dynamic-slice_fusion.7
  394.2 1.2 constant_dynamic-slice_fusion.7
  401.0 1.2 constant_dynamic-slice_fusion.7
  407.7 1.2 constant_dynamic-slice_fusion.7
  414.5 1.2 constant_dynamic-slice_fusion.7
  448.1 1.2 constant_dynamic-slice_fusion.7
  703.4 1.2 constant_dynamic-slice_fusion.7
  750.4 1.2 constant_dynamic-slice_fusion.7
  757.1 1.2 constant_dynamic-slice_fusion.7
  824.3 1.2 constant_dynamic-slice_fusion.7
  958.8 1.2 constant_dynamic-slice_fusion.7
  1012.5 1.2 constant_dynamic-slice_fusion.7
  1077.4 1.5 copy.33
  1078.9 1.5 copy.34
  1080.4 736.8 %reduce-scatter.2.cloned.1.call-done = f32[1,16,56,128]{3,2,1,0:T(8,128)} async-done(((f32[128,16,56,128]{3,2,1,0:T(8,128)}), f32[1,16,56,128]{3,2,1,0:T(8,128)}) %reduce-scatter.2.cloned.1.call-update) | async-done | bytes 458768 | tf_op jit(solution)/shard_map/reduce_scatter | solution.py:53
  1817.2 1.8 multiply_convert_fusion
  (2026 shorter events, 812.4 us)
Async XLA Ops:
  7.2 108.2 %all-gather.4.cloned.1.call-start = ((), (), s32[]{:S(2)}) async-start(), calls=%async_computation.1 | async-start | bytes 29589504 | tf_op jit(solution)/shard_map/all_gather | solution.py:47
  7.9 209.2 %all-gather.6.cloned.1.call-start = ((), (), s32[]{:S(2)}) async-start(), calls=%async_computation.2 | async-start | bytes 29589504 | tf_op jit(solution)/shard_map/all_gather | solution.py:48
  8.6 1808.5 %reduce-scatter.2.cloned.1.call-start = ((), (), s32[]{:S(2)}) async-start(), calls=%async_computation.3 | async-start | bytes 59179008 | tf_op jit(solution)/shard_map/reduce_scatter | solution.py:53
  10.0 41.2 %copy-start.2 = (f32[1,16,56]{2,1,0:T(8,128)S(1)}, f32[1,16,56]{2,1,0:T(8,128)}, u32[]{:S(2)}) copy-start(f32[1,16,56]{2,1,0:T(8,128)} %param.12) | copy-start | bytes 10756
  219.4 1.7 copy-start
  239.6 1.7 copy-start
  246.3 1.7 copy-start
  259.8 1.7 copy-start
  266.5 1.7 copy-start
  279.9 1.7 copy-start
  293.4 1.7 copy-start
  313.5 1.7 copy-start
  340.4 1.7 copy-start
  360.7 1.7 copy-start
  367.4 1.7 copy-start
  374.1 1.7 copy-start
  380.8 1.7 copy-start
  387.5 1.7 copy-start
  407.7 1.7 copy-start
  441.3 1.7 copy-start
  448.1 1.7 copy-start
  468.2 1.7 copy-start
  481.6 1.7 copy-start
  508.5 1.7 copy-start
  528.6 1.7 copy-start
  535.3 1.7 copy-start
  555.5 1.7 copy-start
  562.2 1.7 copy-start
  568.9 1.7 copy-start
  589.1 1.7 copy-start
  609.3 1.7 copy-start
  629.4 1.7 copy-start
  636.1 1.7 copy-start
  642.9 1.7 copy-start
  656.3 1.7 copy-start
  663.1 1.7 copy-start
  689.9 1.7 copy-start
  710.1 1.7 copy-start
  716.8 1.7 copy-start
  730.2 1.7 copy-start
  757.1 1.7 copy-start
  770.5 1.7 copy-start
  797.4 1.7 copy-start
  810.9 1.7 copy-start
  824.3 1.7 copy-start
  898.2 1.7 copy-start
  911.7 1.7 copy-start
  918.4 1.7 copy-start
  (85 other events, 140.0 us)
Sparse Core Ops, SparseCore 0:
  10.9 104.3 all-gather.3
  118.3 98.7 all-gather.5
  1077.5 739.6 reduce-scatter.1
where the time goes:
time: 1840 us; the launch traced here: 1830 us
  waiting for transfers between devices  869 us (47%)
  local copies, waits for them, and re-layouts  470 us (26%)
  matrix products  290 us (16%)
  other arithmetic  101 us (5%)
  blocking collectives  74.4 us (4%)
    reduce_scatter x1, waiting for transfers between devices, per_device(): dq_seg = lax.psum_scatter(parts_q, 'cp', scatter_dimension=0) * score_scale  737 us
    dynamic_slice x640, local copies, waits for them, and re-layouts, per_device(): lax.scan(source_step, kv_acc, (q_all, do_all, lse_all, delta_all, q_starts))  345 us
    dynamic_update_slice x128, local copies, waits for them, and re-layouts, per_device(): lax.scan(source_step, kv_acc, (q_all, do_all, lse_all, delta_all, q_starts))  119 us
    all_gather x1, waiting for transfers between devices, per_device(): do_all = lax.all_gather(grad_out[seg_idx], 'cp')  102 us
    add x128, other arithmetic, tile_backward(): q_pos = q_start + jnp.arange(q_tile.shape[0])  88 us
    dot_general x128, matrix products, tile_backward(): jnp.einsum('hqk,qhd->khd', weights.astype(jnp.bfloat16), do_tile, preferr...  68.4 us
    dot_general x128, matrix products, tile_backward(): jnp.einsum('qhd,khd->hqk', q_tile, key_tile, preferred_element_type=jnp.f...  61.3 us
    dot_general x128, matrix products, tile_backward(): jnp.einsum('qhd,khd->hqk', do_tile, value_tile, preferred_element_type=jn...  60.8 us
  transfers between devices with their start and end apart: 3, of which 3 were waited for; matrix products, arithmetic and copies ran while one was open for 0% of the time, Pallas kernels for 0%

commit v1 on v0

v1 whole, which is shorter than its diff:
```python
import functools

import jax
import jax.numpy as jnp
from jax import lax
from jax.experimental import pallas as pl
from jax.experimental.pallas import tpu as pltpu
from jax.sharding import PartitionSpec as P

MESH = pl.DeviceIdType.MESH
CHUNK = 8
LOG2E = 1.4426950408889634


def grid_of(n_chips):
    return {64: (4, 4, 4), 8: (2, 2, 2)}[n_chips]


def rank_of(chip):
    block, place = lax.div(chip, 8), lax.rem(chip, 8)
    z, half = lax.div(block, 2), lax.rem(block, 2)
    idle = lax.rem(z, 2) * 4 + lax.rem(z + half, 4)
    return lax.rem(place + 15 - idle, 8)


def head_of(chip):
    return lax.div(chip, 8) * 7 + rank_of(chip)


def shifted(chip, r, dims, sign):
    nz, ny, nx = dims
    z, y, x = lax.div(chip, ny * nx), lax.rem(lax.div(chip, nx), ny), lax.rem(chip, nx)
    rz, ry, rx = lax.div(r, ny * nx), lax.rem(lax.div(r, nx), ny), lax.rem(r, nx)
    z = lax.rem(z + sign * rz + nz, nz)
    y = lax.rem(y + sign * ry + ny, ny)
    x = lax.rem(x + sign * rx + nx, nx)
    return (z * ny + y) * nx + x


def kernel(n_chips, prefix0, scale, qd_ref, aux_ref, kv_ref, dq_out, dkv_out, qd_buf, aux_buf, kv_buf, row_buf, kpos_buf,
           stage, dqt_acc, dqt_part, dq_stage, qd_send, qd_recv, aux_send, aux_recv, kv_send, kv_recv, pair_send, pair_recv,
           dkv_send, dkv_recv, dq_send, dq_recv, own):
    dims = grid_of(n_chips)
    me = lax.axis_index("cp")
    chip, core = lax.div(me, 2), lax.rem(me, 2)
    partner = (0, chip * 2 + 1 - core)
    q_local = qd_buf.shape[3]
    key_local = kv_buf.shape[2]
    n_chunks = n_chips // CHUNK
    q_blocks = n_chips // 16 if n_chips >= 16 else 1
    q_chips = n_chips // q_blocks
    block = q_chips * q_local
    rows = CHUNK * key_local

    def send_q(r, carry):
        dst = shifted(chip, r, dims, 1)

        @pl.when(rank_of(dst) < 7)
        def _():
            h = head_of(dst)
            there = (0, dst * 2 + core)
            pltpu.make_async_remote_copy(qd_ref.at[h], qd_buf.at[0, chip], qd_send, qd_recv, device_id=there, device_id_type=MESH).start()
            pltpu.make_async_remote_copy(aux_ref.at[h], aux_buf.at[0, chip], aux_send, aux_recv, device_id=there, device_id_type=MESH).start()

        return carry

    def send_kv(r, carry):
        dst = shifted(chip, r, dims, 1)

        @pl.when(rank_of(dst) < 7)
        def _():
            there = (0, dst * 2 + core)
            pltpu.make_async_remote_copy(kv_ref.at[head_of(dst)], kv_buf.at[r], kv_send, kv_recv.at[lax.div(r, CHUNK)],
                                         device_id=there, device_id_type=MESH).start()

        return carry

    lax.fori_loop(1, n_chips, send_q, 0)
    lax.fori_loop(1, n_chips, send_kv, 0)
    active = rank_of(chip) < 7

    def wait_bytes(ref, sem):
        pltpu.make_async_copy(ref, ref, sem).wait()

    @pl.when(active)
    def _():
        my_head = head_of(chip)
        qd_buf[0, chip] = qd_ref[my_head]
        aux_buf[0, chip] = aux_ref[my_head]
        kv_buf[0] = kv_ref[my_head]
        wait_bytes(qd_buf.at[0, pl.ds(0, n_chips - 1)], qd_recv)
        wait_bytes(aux_buf.at[0, pl.ds(0, n_chips - 1)], aux_recv)
        qd_pair = pltpu.make_async_remote_copy(qd_buf.at[0], qd_buf.at[1], pair_send.at[0], pair_recv.at[0], device_id=partner, device_id_type=MESH)
        aux_pair = pltpu.make_async_remote_copy(aux_buf.at[0], aux_buf.at[1], pair_send.at[1], pair_recv.at[1], device_id=partner, device_id_type=MESH)
        qd_pair.start()
        aux_pair.start()

        def make_rows(half):
            for g in range(n_chips // 8):
                row_buf[half, g] = jnp.sum(aux_buf[half, pl.ds(g * 8, 8)], axis=0)

        make_rows(0)
        dqt_acc[...] = jnp.zeros_like(dqt_acc)

        def step(i, carry):
            j, half = lax.div(i, 2), lax.rem(i, 2)

            @pl.when(half == 0)
            def _():
                @pl.when(j == 0)
                def _():
                    wait_bytes(kv_buf.at[pl.ds(1, CHUNK - 1)], kv_recv.at[0])

                @pl.when(j > 0)
                def _():
                    wait_bytes(kv_buf.at[pl.ds(j * CHUNK, CHUNK)], kv_recv.at[j])

                stage[pl.ds(j * CHUNK, CHUNK)] = jnp.zeros((CHUNK,) + stage.shape[1:], jnp.float32)
                for k in range(CHUNK):
                    source = shifted(chip, j * CHUNK + k, dims, -1)
                    first = (source * 2 + core) * key_local - prefix0
                    kpos_buf[pl.ds(k * key_local, key_local)] = first + lax.broadcasted_iota(jnp.int32, (key_local, 128), 0)

            @pl.when(i == 1)
            def _():
                qd_pair.wait()
                aux_pair.wait()
                make_rows(1)

            q_core = lax.rem(core + half, 2)
            keys = kv_buf[pl.ds(j * CHUNK, CHUNK), 0].reshape(rows, 128)
            values = kv_buf[pl.ds(j * CHUNK, CHUNK), 1].reshape(rows, 128)
            keys_t = keys.T

            def q_step(b, carry):
                q = qd_buf[half, pl.ds(b * q_chips, q_chips), 0].reshape(block, 128)
                do = qd_buf[half, pl.ds(b * q_chips, q_chips), 1].reshape(block, 128)
                aux = [row_buf[half, b * (q_chips // 8) + g] for g in range(q_chips // 8)]
                lse2 = jnp.concatenate([a[0:1] for a in aux], axis=1) * LOG2E
                delta = jnp.concatenate([a[1:2] for a in aux], axis=1)
                lane = lax.broadcasted_iota(jnp.int32, (1, block), 1)
                qpos = ((b * q_chips + lax.div(lane, q_local)) * 2 + q_core) * q_local + lax.rem(lane, q_local)
                kpos = jnp.concatenate([kpos_buf[...]] * (block // 128), axis=1)
                s = lax.dot_general(keys, q, (((1,), (1,)), ((), ())), preferred_element_type=jnp.float32)
                p = jnp.where(kpos <= qpos, jnp.exp2(s * (scale * LOG2E) - lse2), 0.0)
                dp = lax.dot_general(values, do, (((1,), (1,)), ((), ())), preferred_element_type=jnp.float32)
                ds = (p * (dp - delta)).astype(jnp.bfloat16)
                dv = jnp.dot(p.astype(jnp.bfloat16), do, preferred_element_type=jnp.float32)
                dk = jnp.dot(ds, q, preferred_element_type=jnp.float32)
                stage[pl.ds(j * CHUNK, CHUNK), 0] += dk.reshape(CHUNK, key_local, 128)
                stage[pl.ds(j * CHUNK, CHUNK), 1] += dv.reshape(CHUNK, key_local, 128)
                dqt_acc[half, b] += jnp.dot(keys_t, ds, preferred_element_type=jnp.float32)
                return carry

            lax.fori_loop(0, q_blocks, q_step, 0)

            @pl.when(half == 1)
            def _():
                stage[pl.ds(j * CHUNK, CHUNK), 0] = stage[pl.ds(j * CHUNK, CHUNK), 0] * scale

                @pl.when(j == 0)
                def _():
                    pltpu.make_async_copy(stage.at[0], dkv_out.at[my_head], own.at[0]).start()

                def send_back(r, carry):
                    source = shifted(chip, r, dims, -1)
                    pltpu.make_async_remote_copy(stage.at[r], dkv_out.at[my_head], dkv_send, dkv_recv,
                                                 device_id=(0, source * 2 + core), device_id_type=MESH).start()
                    return carry

                lax.fori_loop(jnp.maximum(j * CHUNK, 1), j * CHUNK + CHUNK, send_back, 0)

            return carry

        lax.fori_loop(0, 2 * n_chunks, step, 0)

        dq_pair = pltpu.make_async_remote_copy(dqt_acc.at[1], dqt_part, pair_send.at[2], pair_recv.at[2], device_id=partner, device_id_type=MESH)
        dq_pair.start()
        dq_pair.wait()
        for b in range(q_blocks):
            dq = ((dqt_acc[0, b] + dqt_part[b]) * scale).T
            dq_stage[pl.ds(b * q_chips, q_chips)] = dq.astype(jnp.bfloat16).reshape(q_chips, q_local, 128)

        def send_dq(r, carry):
            source = shifted(chip, r, dims, -1)
            pltpu.make_async_remote_copy(dq_stage.at[source], dq_out.at[my_head], dq_send, dq_recv,
                                         device_id=(0, source * 2 + core), device_id_type=MESH).start()
            return carry

        own_dq = pltpu.make_async_copy(dq_stage.at[chip], dq_out.at[my_head], own.at[1])
        own_dq.start()
        lax.fori_loop(1, n_chips, send_dq, 0)
        wait_bytes(stage.at[pl.ds(1, n_chips - 1)], dkv_send)
        wait_bytes(dq_stage.at[pl.ds(1, n_chips - 1)], dq_send)
        pltpu.make_async_copy(stage.at[0], dkv_out.at[my_head], own.at[0]).wait()
        own_dq.wait()

    def finish(count):
        first = pl.ds(0, count)
        wait_bytes(qd_ref.at[first], qd_send)
        wait_bytes(aux_ref.at[first], aux_send)
        wait_bytes(kv_ref.at[first], kv_send)
        wait_bytes(dkv_out.at[first], dkv_recv)
        wait_bytes(dq_out.at[first], dq_recv)

    n_heads = qd_ref.shape[0]

    @pl.when(active)
    def _():
        finish(n_heads - 1)

    @pl.when(jnp.logical_not(active))
    def _():
        finish(n_heads)


def solution(mesh):
    cp_size = mesh.shape["cp"]
    n_chips = cp_size // 2
    spec_q = P(None, "cp", "heads", None)
    spec_kv = P("cp", "heads", None)
    spec_lse = P(None, "cp", "heads")

    def per_device(queries, key_vecs, value_vecs, attn_out, log_sum_exp, grad_out):
        _, q_local, n_heads, head_dim = queries.shape
        key_local = key_vecs.shape[0]
        prefix0 = (key_local - q_local) * cp_size
        scale = head_dim ** -0.5
        place = lax.rem(lax.div(lax.axis_index("cp"), 2), 8)
        row_delta = jnp.einsum("qhd,qhd->qh", grad_out[0], attn_out[0], preferred_element_type=jnp.float32)
        aux = jnp.stack([log_sum_exp[0].T, row_delta.T], axis=1)
        lanes = jnp.arange(128) // q_local
        aux = jnp.where(lanes == place, jnp.tile(aux, (1, 1, 128 // q_local)), 0.0)
        qd = jnp.stack([queries[0], grad_out[0]]).transpose(2, 0, 1, 3)
        kv = jnp.stack([key_vecs, value_vecs]).transpose(2, 0, 1, 3)
        q_blocks = n_chips // 16 if n_chips >= 16 else 1
        block = n_chips // q_blocks * q_local
        n_chunks = n_chips // CHUNK
        bf16, f32 = jnp.bfloat16, jnp.float32
        dma = pltpu.SemaphoreType.DMA
        dq, dkv = pl.pallas_call(
            functools.partial(kernel, n_chips, prefix0, scale),
            name="exchange_and_backward",
            out_shape=(jax.ShapeDtypeStruct((n_heads, q_local, head_dim), bf16), jax.ShapeDtypeStruct((n_heads, 2, key_local, head_dim), f32)),
            in_specs=[pl.BlockSpec(memory_space=pltpu.VMEM)] * 3,
            out_specs=[pl.BlockSpec(memory_space=pl.ANY)] * 2,
            scratch_shapes=[
                pltpu.VMEM((2, n_chips, 2, q_local, head_dim), bf16),
                pltpu.VMEM((2, n_chips, 2, 128), f32),
                pltpu.VMEM((n_chips, 2, key_local, head_dim), bf16),
                pltpu.VMEM((2, n_chips // 8, 2, 128), f32),
                pltpu.VMEM((CHUNK * key_local, 128), jnp.int32),
                pltpu.VMEM((n_chips, 2, key_local, head_dim), f32),
                pltpu.VMEM((2, q_blocks, head_dim, block), f32),
                pltpu.VMEM((q_blocks, head_dim, block), f32),
                pltpu.VMEM((n_chips, q_local, head_dim), bf16),
                dma, dma, dma, dma, dma, dma((n_chunks,)), dma((3,)), dma((3,)), dma, dma, dma, dma, dma((2,)),
            ],
            compiler_params=pltpu.CompilerParams(has_side_effects=True, vmem_limit_bytes=56 * 1024 * 1024),
        )(qd, aux, kv)
        grad_q = dq.transpose(1, 0, 2)[None]
        return grad_q, dkv[:, 0].transpose(1, 0, 2), dkv[:, 1].transpose(1, 0, 2)

    return jax.shard_map(per_device, mesh=mesh, in_specs=(spec_q, spec_kv, spec_kv, spec_q, spec_lse, spec_q), out_specs=(spec_q, spec_kv, spec_kv), check_vma=False)
```

time: 1840 us -> 105 us (0.06)
  the two profiles are of different devices: /device:TPU:0 before, /device:TPU:7 now
where the time goes in v1:
time: 105 us; the launch traced here: 104 us
  Pallas kernels  90.9 us (87%)
  local copies, waits for them, and re-layouts  7.93 us (8%)
  other arithmetic  4.73 us (5%)
    pallas_call x1, Pallas kernels, per_device(): pl.pallas_call(functools.partial(kernel, n_chips, prefix0, scale), name='...  90.9 us
    unnamed x11, local copies, waits for them, and re-layouts  5.71 us

profile of v1, /device:TPU:7, one launch (start us, length us, event | category | flops | bytes accessed | tf_op | source)
XLA Modules:
  0.0 104.3 jit_solution(617677364028227446)
XLA Ops:
  0.6 0.0 copy-start
  0.7 0.0 copy-start.1
  0.7 0.0 copy-start.2
  0.7 1.4 %fusion = f32[56,16]{0,1:T(8,128)S(1)} fusion(bf16[1,16,56,128]{3,2,1,0:T(8,128)(2,1)} %param.11, bf16[1,16,56,128]{3,2,1,0:T(8,128)(2,1)} %param.9), kind=kLoop, calls=%fused_computation.7 | loop fusion | flops 457856 | bytes 462336 | tf_op jit(solution)/shard_map/qhd,qhd->qh/dot_general | solution.py:230
  2.0 0.7 pad_maximum_fusion
  2.8 0.1 copy.19
  2.9 0.7 broadcast_select_fusion.aux_ref
  3.5 1.0 copy.17
  4.5 0.0 copy-done
  4.5 0.8 maximum_bitcast_fusion.1.qd_ref
  5.3 0.0 copy-done.1
  5.3 0.0 copy-done.2
  5.3 0.2 copy_bitcast_fusion
  5.5 1.2 %maximum_bitcast_fusion.kv_ref = bf16[56,2,48,128]{3,2,1,0:T(8,128)(2,1)} fusion(bf16[1,48,56,128]{3,1,0,2:T(8,128)(2,1)S(1)} %get-tuple-element.15, bf16[1,48,56,128]{3,1,0,2:T(8,128)(2,1)S(1)} %get-tuple-element.16), kind=kLoop, calls=%fused_computation | loop fusion | flops 688128 | bytes 2752512 | tf_op jit(solution)/shard_map/transpose | solution.py:235
  6.7 90.9 %exchange_and_backward.1 = (bf16[56,16,128]{2,1,0:T(8,128)(2,1)}, f32[56,2,48,128]{3,2,1,0:T(8,128)}) custom-call(bf16[56,2,16,128]{3,2,1,0:T(8,128)(2,1)} %maximum_bitcast_fusion.1.qd_ref, f32[56,2,128]{2,1,0:T(2,128)} %broadcast_select_fusion.aux_ref, bf16[56,2,48,128]{3,2,1,0:T(8,128)(2,1)} %maximum_bitcast_fusion.kv_ref), custom_call_target="tpu_custom_call" | custom-call | tf_op jit(solution)/shard_map/exchange_and_backward/pallas_call | solution.py:241
  97.7 1.7 %copy.22 = bf16[1,16,56,128]{3,2,1,0:T(8,128)(2,1)} copy(bf16[1,16,56,128]{3,1,2,0:T(8,128)(2,1)} %bitcast.35) | data formatting | bytes 458752
  99.3 1.9 %slice_bitcast_fusion = (f32[48,56,128]{2,0,1:T(8,128)S(1)}, f32[48,56,128]{2,0,1:T(8,128)S(1)}) fusion(f32[56,2,48,128]{3,2,1,0:T(8,128)} %get-tuple-element.6), kind=kLoop, calls=%fused_computation.1 | loop fusion | bytes 5505024 | tf_op jit(solution)/shard_map/transpose | solution.py:262
  101.3 1.5 %copy.24 = f32[48,56,128]{2,1,0:T(8,128)} copy(f32[48,56,128]{2,0,1:T(8,128)S(1)} %get-tuple-element.13) | data formatting | bytes 2752512
  102.8 1.5 %copy.23 = f32[48,56,128]{2,1,0:T(8,128)} copy(f32[48,56,128]{2,0,1:T(8,128)S(1)} %get-tuple-element.14) | data formatting | bytes 2752512
  (3 shorter events, 0.1 us)
Async XLA Ops:
  0.6 3.9 %copy-start = (bf16[1,16,56,128]{3,2,1,0:T(8,128)(2,1)S(1)}, bf16[1,16,56,128]{3,2,1,0:T(8,128)(2,1)}, u32[]{:S(2)}) copy-start(bf16[1,16,56,128]{3,2,1,0:T(8,128)(2,1)} %param.11) | copy-start | bytes 688132
  0.7 4.7 %copy-start.1 = (bf16[48,56,128]{2,1,0:T(8,128)(2,1)S(1)}, bf16[48,56,128]{2,1,0:T(8,128)(2,1)}, u32[]{:S(2)}) copy-start(bf16[48,56,128]{2,1,0:T(8,128)(2,1)} %param.8) | copy-start | bytes 2064388
  0.7 4.7 %copy-start.2 = (bf16[48,56,128]{2,1,0:T(8,128)(2,1)S(1)}, bf16[48,56,128]{2,1,0:T(8,128)(2,1)}, u32[]{:S(2)}) copy-start(bf16[48,56,128]{2,1,0:T(8,128)(2,1)} %param.7) | copy-start | bytes 2064388

commit v2 on v0

v2 whole, which is shorter than its diff:
```python
import functools

import jax
import jax.numpy as jnp
from jax import lax
from jax.experimental import pallas as pl
from jax.experimental.pallas import tpu as pltpu
from jax.sharding import PartitionSpec as P

MESH = pl.DeviceIdType.MESH
GROUPS = 4
LINE_AXIS = (0, 1, 2, 0)
FIRST_AXIS = (1, 2, 0, 2)
SECOND_AXIS = (2, 0, 1, 1)
LOG2E = 1.4426950408889634
FORWARD_LAG = 2
STORE_LAG = 4
F32, BF16 = jnp.float32, jnp.bfloat16


def pick(table, g):
    if isinstance(g, int):
        return table[g]
    value = table[-1]
    for k in range(len(table) - 1):
        value = jnp.where(g == k, table[k], value)
    return value


def rank_at(n, a, b):
    size = 8 if n == 4 else 4
    pos = a * n + b
    block, place = lax.div(pos, size), lax.rem(pos, size)
    rank = lax.rem(place + 2 * size - 1 - block * 2, size)
    return block * (size - 1) + rank, rank < size - 1


class Spot:
    def __init__(self, n, coords, chip, core, g):
        strides = (n * n, n, 1)
        self.n, self.chip, self.core = n, chip, core
        self.s_line, self.s_a, self.s_b = (pick([strides[t[k]] for k in range(GROUPS)], g) for t in (LINE_AXIS, FIRST_AXIS, SECOND_AXIS))
        self.line, self.a, self.b = (pick([coords[t[k]] for k in range(GROUPS)], g) for t in (LINE_AXIS, FIRST_AXIS, SECOND_AXIS))

    def turn(self, c, d):
        return lax.rem(c + d + self.n, self.n)

    def at(self, a=0, b=0, line=0):
        return (self.chip + (self.turn(self.a, a) - self.a) * self.s_a + (self.turn(self.b, b) - self.b) * self.s_b
                + (self.turn(self.line, line) - self.line) * self.s_line)

    def device(self, a=0, b=0, line=0):
        return (0, self.at(a, b, line) * 2 + self.core)

    def rank(self, a=0, b=0):
        return rank_at(self.n, self.turn(self.a, a), self.turn(self.b, b))


def kernel(n, prefix0, scale, n_heads, q_in, k_in, v_in, o_in, lse_in, do_in, dq_out, dk_out, dv_out,
           q_raw, k_raw, v_raw, o_raw, lse_raw, do_raw, q_f32, do_f32, k_f32, v_f32, lse_pad, aux_rows,
           q_src, aux_src, kv_src, qd, aux, rows, kv1, kv2, kpos_buf, res, ret1, ret2, dqt, part, line_sum, dq_src, dq_got,
           dq_f32, dk_f32, dv_f32, dq_bf,
           in_sem, q_send, q_recv, aux_send, aux_recv, ql_send, ql_recv, al_send, al_recv, pair_send, pair_recv, k1_send, k1_recv,
           k2_send, k2_recv, r1_send, r1_recv, r2_send, r2_recv, part_send, part_recv, ls_send, ls_recv, dq_send, dq_recv, out_sem):
    me = lax.axis_index("cp")
    chip, core = lax.div(me, 2), lax.rem(me, 2)
    coords = (lax.div(chip, n * n), lax.rem(lax.div(chip, n), n), lax.rem(chip, n))
    partner = (0, chip * 2 + 1 - core)
    spots = [Spot(n, coords, chip, core, g) for g in range(GROUPS)]
    holds = [s.rank()[1] for s in spots]
    heads = n_heads // GROUPS
    q_local, key_local = q_src.shape[3], kv_src.shape[4]
    plane = n * n
    unit_rows = min(8, plane)
    width = unit_rows * q_local
    block = plane * q_local
    n_rows = block // width
    keys_in = n * key_local

    def remote(src, dst, send, recv, device):
        return pltpu.make_async_remote_copy(src, dst, send, recv, device_id=device, device_id_type=MESH)

    def wait_bytes(ref, sem):
        pltpu.make_async_copy(ref, ref, sem).wait()

    loads = [pltpu.make_async_copy(a, b, in_sem.at[k]) for k, (a, b) in enumerate(
        [(q_in, q_raw), (do_in, do_raw), (o_in, o_raw), (lse_in, lse_raw), (k_in, k_raw), (v_in, v_raw)])]
    for copy in loads:
        copy.start()

    barrier = pltpu.get_barrier_semaphore()
    met = 1
    pl.semaphore_signal(barrier, inc=1, device_id=partner, device_id_type=MESH)
    for g, spot in enumerate(spots[:3]):
        for a in range(n):
            for b in range(1, n):
                pl.semaphore_signal(barrier, inc=1, device_id=spot.device(a, b), device_id_type=MESH)
                met += 1

    def widen(src, dst, count):
        per = n_heads * 4

        def go(t, carry):
            at = pl.ds(pl.multiple_of(t * per, 8), per)
            dst[at] = src[at].astype(F32)
            return carry

        lax.fori_loop(0, count // 4, go, 0)

    for copy in loads[:4]:
        copy.wait()
    widen(q_raw, q_f32, q_local)
    widen(do_raw, do_f32, q_local)
    lse_pad[0:q_local, 0:n_heads] = lse_raw[...]
    lse_t = lse_pad[...].T[0:n_heads]
    head_group = lax.div(lax.broadcasted_iota(jnp.int32, (n_heads, 128), 0), heads)
    lane = lax.broadcasted_iota(jnp.int32, (n_heads, 128), 1)
    base = pick([lax.rem(s.b * n + s.a, unit_rows) * q_local for s in spots], head_group)
    row_lse, row_delta = jnp.zeros((n_heads, 128), F32), jnp.zeros((n_heads, 128), F32)
    for t in range(q_local):
        at = pl.ds(t * n_heads, n_heads)
        delta = jnp.sum(do_f32[at] * o_raw[at].astype(F32), axis=1, keepdims=True)
        row_delta = jnp.where(lane == base + t, delta, row_delta)
        row_lse = jnp.where(lane == base + t, lse_t[:, t:t + 1], row_lse)
    aux_rows[0] = row_lse
    aux_rows[1] = row_delta

    def lay_out_q(i, carry):
        g = lax.div(i, plane)
        spot = Spot(n, coords, chip, core, g)
        rank, _ = spot.rank(lax.div(lax.rem(i, plane), n), lax.rem(i, n))
        h = g * heads + lax.rem(rank, heads)
        u = lax.rem(i, plane)
        q_src[g, u, 0] = q_f32[pl.ds(h, q_local, stride=n_heads), :].astype(BF16)
        q_src[g, u, 1] = do_f32[pl.ds(h, q_local, stride=n_heads), :].astype(BF16)
        aux_src[g, u, 0:1] = aux_rows[0, pl.ds(h, 1), :]
        aux_src[g, u, 1:2] = aux_rows[1, pl.ds(h, 1), :]
        return carry

    lax.fori_loop(0, GROUPS * plane, lay_out_q, 0)
    for copy in loads[4:]:
        copy.wait()
    widen(k_raw, k_f32, key_local)
    widen(v_raw, v_f32, key_local)

    def lay_out_kv(i, carry):
        g = lax.div(i, plane)
        spot = Spot(n, coords, chip, core, g)
        d1, d2 = lax.div(lax.rem(i, plane), n), lax.rem(i, n)
        rank, _ = spot.rank(d1, d2)
        h = g * heads + lax.rem(rank, heads)
        kv_src[g, d1, d2, 0] = k_f32[pl.ds(h, key_local, stride=n_heads), :].astype(BF16)
        kv_src[g, d1, d2, 1] = v_f32[pl.ds(h, key_local, stride=n_heads), :].astype(BF16)
        return carry

    lax.fori_loop(0, GROUPS * plane, lay_out_kv, 0)
    pl.semaphore_wait(barrier, met)

    def send_q():
        def go(i, carry):
            g, u = lax.div(i, plane), lax.rem(i, plane)
            spot = Spot(n, coords, chip, core, g)
            d1, d2 = lax.div(u, n), lax.rem(u, n)

            @pl.when(jnp.logical_and(u > 0, spot.rank(d1, d2)[1]))
            def _():
                there = spot.device(d1, d2)
                remote(q_src.at[g, u], qd.at[g, 0, spot.line, spot.b, spot.a], q_send.at[g], q_recv.at[g], there).start()
                remote(aux_src.at[g, u], aux.at[g, 0, spot.line, spot.b, spot.a], aux_send.at[g], aux_recv.at[g], there).start()

            return carry

        lax.fori_loop(0, GROUPS * plane, go, 0)

    def k_first(g):
        for d in range(1, n):
            remote(kv_src.at[g, d], kv1.at[g, d], k1_send.at[g], k1_recv.at[g], spots[g].device(a=d)).start()

    def k_second(g, own):
        for d in range(1, n):
            @pl.when(spots[g].rank(b=d)[1])
            def _():
                there = spots[g].device(b=d)
                if own:
                    remote(kv_src.at[g, 0, d], kv2.at[g, d, 0], k2_send.at[g, d], k2_recv.at[g, d], there).start()
                else:
                    remote(kv1.at[g, pl.ds(1, n - 1), d], kv2.at[g, d, pl.ds(1, n - 1)], k2_send.at[g, d], k2_recv.at[g, d], there).start()

    def q_line(g):
        for d in range(1, n):
            there = spots[g].device(line=d)
            remote(qd.at[g, 0, spots[g].line], qd.at[g, 0, spots[g].line], ql_send.at[g], ql_recv.at[g], there).start()
            remote(aux.at[g, 0, spots[g].line], aux.at[g, 0, spots[g].line], al_send.at[g], al_recv.at[g], there).start()

    send_q()
    for g in range(GROUPS):
        k_first(g)
    for g in range(GROUPS):
        k_second(g, True)
    for g, spot in enumerate(spots):
        @pl.when(holds[g])
        def _():
            qd[g, 0, spot.line, spot.b, spot.a] = q_src[g, 0]
            aux[g, 0, spot.line, spot.b, spot.a] = aux_src[g, 0]
            wait_bytes(q_src.at[g, pl.ds(1, plane - 1)], q_recv.at[g])
            wait_bytes(aux_src.at[g, pl.ds(1, plane - 1)], aux_recv.at[g])
            q_line(g)

    for g in range(GROUPS):
        wait_bytes(kv1.at[g, pl.ds(1, n - 1)], k1_recv.at[g])
        k_second(g, False)

    def pair_copies(g):
        return (remote(qd.at[g, 0], qd.at[g, 1], pair_send.at[0, g], pair_recv.at[0, g], partner),
                remote(aux.at[g, 0], aux.at[g, 1], pair_send.at[1, g], pair_recv.at[1, g], partner))

    def share_queries(g):
        wait_bytes(qd.at[g, 0, pl.ds(0, n - 1)], ql_recv.at[g])
        wait_bytes(aux.at[g, 0, pl.ds(0, n - 1)], al_recv.at[g])
        for copy in pair_copies(g):
            copy.start()

    @pl.when(holds[0])
    def _():
        share_queries(0)

    n_chunks = GROUPS * n

    def chunk_of(i):
        g = lax.div(i, n)
        return g, lax.rem(lax.rem(i, n) + jnp.where(g == GROUPS - 1, 1, 0), n)

    def compute(i):
        g, o2 = chunk_of(i)
        spot = Spot(n, coords, chip, core, g)

        @pl.when(lax.rem(i, n) == 0)
        def _():
            for copy in pair_copies(g):
                copy.wait()
            for half in range(2):
                for l in range(n):
                    units = aux[g, half, l].reshape(n_rows, unit_rows, 2, 128)
                    rows[half, l] = jnp.sum(units, axis=1)
            dqt[g] = jnp.zeros(dqt.shape[1:], F32)

        @pl.when(o2 == 0)
        def _():
            kv2[g, 0, 0] = kv_src[g, 0, 0]
            for o1 in range(1, n):
                kv2[g, 0, o1] = kv1[g, o1, 0]

        @pl.when(o2 > 0)
        def _():
            wait_bytes(kv2.at[g, o2], k2_recv.at[g, o2])

        for o1 in range(n):
            first = (spot.at(a=-o1, b=-o2) * 2 + core) * key_local - prefix0
            kpos_buf[pl.ds(o1 * key_local, key_local)] = first + lax.broadcasted_iota(jnp.int32, (key_local, 128), 0)
        keys = kv2[g, o2, :, 0].reshape(keys_in, 128)
        values = kv2[g, o2, :, 1].reshape(keys_in, 128)
        keys_t = keys.T
        res[g, o2] = jnp.zeros(res.shape[2:], F32)

        def q_step(s, carry):
            half = lax.rem(s, 2)
            l = spot.turn(spot.line, 1 + lax.div(s, 2))
            q = qd[g, half, l, :, :, 0].reshape(block, 128)
            do = qd[g, half, l, :, :, 1].reshape(block, 128)
            lse2 = jnp.concatenate([rows[half, l, r, 0:1, 0:width] for r in range(n_rows)], axis=1) * LOG2E
            delta = jnp.concatenate([rows[half, l, r, 1:2, 0:width] for r in range(n_rows)], axis=1)
            lanes = lax.broadcasted_iota(jnp.int32, (1, block), 1)
            unit = lax.div(lanes, q_local)
            q_chip = l * spot.s_line + lax.div(unit, n) * spot.s_b + lax.rem(unit, n) * spot.s_a
            qpos = (q_chip * 2 + lax.rem(core + half, 2)) * q_local + lax.rem(lanes, q_local)
            kpos = jnp.concatenate([kpos_buf[...]] * n_rows, axis=1)[:, 0:block]
            s_ = lax.dot_general(keys, q, (((1,), (1,)), ((), ())), preferred_element_type=F32)
            p = jnp.where(kpos <= qpos, jnp.exp2(s_ * (scale * LOG2E) - lse2), 0.0)
            dp = lax.dot_general(values, do, (((1,), (1,)), ((), ())), preferred_element_type=F32)
            ds = (p * (dp - delta)).astype(BF16)
            res[g, o2, :, 0] += jnp.dot(ds, q, preferred_element_type=F32).reshape(n, key_local, 128)
            res[g, o2, :, 1] += jnp.dot(p.astype(BF16), do, preferred_element_type=F32).reshape(n, key_local, 128)
            dqt[g, half, l] += jnp.dot(keys_t, ds, preferred_element_type=F32)
            return carry

        lax.fori_loop(0, 2 * n, q_step, 0)
        res[g, o2, :, 0] = res[g, o2, :, 0] * scale

    def part_copy(g):
        return remote(dqt.at[g, 1], part.at[g], part_send.at[g], part_recv.at[g], partner)

    def line_copy(g, spot, d):
        return remote(dqt.at[g, 0, spot.turn(spot.line, d)], line_sum.at[g, n - 1 - d], ls_send.at[g], ls_recv.at[g], spot.device(line=d))

    def dq_copy(g, spot, u):
        b, a = spot.turn(spot.b, lax.div(u, n)), spot.turn(spot.a, lax.rem(u, n))
        h = g * heads + lax.rem(spot.rank()[0], heads)
        return remote(dq_src.at[g, b * n + a], dq_got.at[h], dq_send.at[g], dq_recv.at[g], spot.device(a=lax.rem(u, n), b=lax.div(u, n)))

    def first_back(g, o2, spot):
        return remote(res.at[g, o2], ret1.at[g, o2], r1_send.at[g, o2], r1_recv.at[g, o2], spot.device(b=-o2))

    def second_back(g, o2, o1, spot, src):
        return remote(src.at[g, o2, o1], ret2.at[g, o2, o1], r2_send.at[g, o2], r2_recv.at[g, o2, o1], spot.device(a=-o1))

    def step(i, carry):
        @pl.when(i < n_chunks)
        def _():
            g, o2 = chunk_of(i)
            spot = Spot(n, coords, chip, core, g)

            @pl.when(spot.rank()[1])
            def _():
                compute(i)

                @pl.when(o2 > 0)
                def _():
                    first_back(g, o2, spot).start()

                @pl.when(o2 == 0)
                def _():
                    for o1 in range(1, n):
                        second_back(g, 0, o1, spot, res).start()

        @pl.when(jnp.logical_and(lax.rem(i, n) == n - 1, i < n_chunks))
        def _():
            g = lax.div(i, n)

            @pl.when(Spot(n, coords, chip, core, g).rank()[1])
            def _():
                part_copy(g).start()

        @pl.when(jnp.logical_and(lax.rem(i, n) == 0, jnp.logical_and(i >= n, i <= n_chunks)))
        def _():
            g = lax.div(i, n) - 1
            spot = Spot(n, coords, chip, core, g)

            @pl.when(spot.rank()[1])
            def _():
                part_copy(g).wait()
                for l in range(n):
                    dqt[g, 0, l] = dqt[g, 0, l] + part[g, l]
                for d in range(1, n):
                    line_copy(g, spot, d).start()

        @pl.when(jnp.logical_and(lax.rem(i, n) == 1, jnp.logical_and(i >= n, i <= n_chunks + 1)))
        def _():
            g = lax.div(i, n) - 1
            spot = Spot(n, coords, chip, core, g)

            @pl.when(spot.rank()[1])
            def _():
                wait_bytes(line_sum.at[g], ls_recv.at[g])
                total = dqt[g, 0, spot.line]
                for d in range(n - 1):
                    total = total + line_sum[g, d]
                dq_src[g] = (total * scale).T.astype(BF16).reshape(plane, q_local, 128)
                h = g * heads + spot.rank()[0]
                dq_got[h] = dq_src[g, spot.b * n + spot.a]

                def go(u, carry):
                    dq_copy(g, spot, u).start()
                    return carry

                lax.fori_loop(1, plane, go, 0)

        @pl.when(jnp.logical_and(lax.rem(i, n) == n - 2, i < n_chunks - n))
        def _():
            g = lax.div(i, n) + 1

            @pl.when(Spot(n, coords, chip, core, g).rank()[1])
            def _():
                share_queries(g)

        j = i - FORWARD_LAG

        @pl.when(jnp.logical_and(j >= 0, j < n_chunks))
        def _():
            g, o2 = chunk_of(j)
            spot = Spot(n, coords, chip, core, g)

            @pl.when(jnp.logical_and(o2 > 0, spot.rank(b=o2)[1]))
            def _():
                wait_bytes(ret1.at[g, o2], r1_recv.at[g, o2])
                for o1 in range(1, n):
                    second_back(g, o2, o1, spot, ret1).start()

        k = i - STORE_LAG

        @pl.when(k >= 0)
        def _():
            g, o2 = chunk_of(k)
            spot = Spot(n, coords, chip, core, g)

            def put(o1, src):
                rank, _ = spot.rank(a=o1, b=o2)
                at = pl.ds(g * heads + rank, key_local, stride=n_heads)
                dk_f32[at, :] = src[g, o2, o1, 0]
                dv_f32[at, :] = src[g, o2, o1, 1]

            for o1 in range(n):
                @pl.when(spot.rank(a=o1, b=o2)[1])
                def _():
                    if o1:
                        wait_bytes(ret2.at[g, o2, o1], r2_recv.at[g, o2, o1])
                        return
                    pl.when(o2 == 0)(lambda: put(0, res))
                    pl.when(o2 > 0)(lambda: put(0, ret1))

            for o1 in range(1, n):
                @pl.when(spot.rank(a=o1, b=o2)[1])
                def _():
                    put(o1, ret2)

        return carry

    lax.fori_loop(0, n_chunks + STORE_LAG, step, 0)

    outs = [pltpu.make_async_copy(dk_f32, dk_out, out_sem.at[0]), pltpu.make_async_copy(dv_f32, dv_out, out_sem.at[1])]
    for copy in outs:
        copy.start()
    for g in range(GROUPS):
        for mine in (False, True):
            @pl.when(holds[g] if mine else jnp.logical_not(holds[g]))
            def _():
                wait_bytes(dq_got.at[pl.ds(0, heads - mine)], dq_recv.at[g])

    def put_dq(h, carry):
        dq_f32[pl.ds(h, q_local, stride=n_heads), :] = dq_got[h].astype(F32)
        return carry

    lax.fori_loop(0, n_heads, put_dq, 0)
    dq_bf[...] = dq_f32[...].astype(BF16)
    dq_copy_out = pltpu.make_async_copy(dq_bf, dq_out, out_sem.at[2])
    dq_copy_out.start()

    for g, spot in enumerate(spots):
        for mine in (False, True):
            @pl.when(holds[g] if mine else jnp.logical_not(holds[g]))
            def _():
                wait_bytes(q_src.at[g, pl.ds(0, heads - mine)], q_send.at[g])
                wait_bytes(aux_src.at[g, pl.ds(0, heads - mine)], aux_send.at[g])
        wait_bytes(kv1.at[g, pl.ds(1, n - 1)], k1_send.at[g])

        @pl.when(holds[g])
        def _():
            wait_bytes(qd.at[g, 0, pl.ds(0, n - 1)], ql_send.at[g])
            wait_bytes(aux.at[g, 0, pl.ds(0, n - 1)], al_send.at[g])
            wait_bytes(line_sum.at[g], ls_send.at[g])
            wait_bytes(dq_src.at[g, pl.ds(1, plane - 1)], dq_send.at[g])
            wait_bytes(res.at[g, 0, pl.ds(1, n - 1)], r2_send.at[g, 0])
            for d in range(1, n):
                wait_bytes(res.at[g, d], r1_send.at[g, d])

        for d in range(1, n):
            @pl.when(spot.rank(b=d)[1])
            def _():
                wait_bytes(kv2.at[g, d], k2_send.at[g, d])
                wait_bytes(res.at[g, d, pl.ds(1, n - 1)], r2_send.at[g, d])

    for copy in outs:
        copy.wait()
    dq_copy_out.wait()


def solution(mesh):
    cp_size = mesh.shape["cp"]
    n = {128: 4, 16: 2}[cp_size]
    spec_q = P(None, "cp", "heads", None)
    spec_kv = P("cp", "heads", None)
    spec_lse = P(None, "cp", "heads")

    def per_device(queries, key_vecs, value_vecs, attn_out, log_sum_exp, grad_out):
        _, q_local, n_heads, dim = queries.shape
        key_local = key_vecs.shape[0]
        prefix0 = (key_local - q_local) * cp_size
        plane, block = n * n, n * n * q_local
        q_rows, k_rows = q_local * n_heads, key_local * n_heads
        unit_rows = min(8, plane)
        dma = pltpu.SemaphoreType.DMA
        g4 = GROUPS
        vmem = pltpu.VMEM
        scratch = [
            vmem((q_rows, dim), BF16), vmem((k_rows, dim), BF16), vmem((k_rows, dim), BF16), vmem((q_rows, dim), BF16),
            vmem((q_local, n_heads), F32), vmem((q_rows, dim), BF16),
            vmem((q_rows, dim), F32), vmem((q_rows, dim), F32), vmem((k_rows, dim), F32), vmem((k_rows, dim), F32),
            vmem((128, 128), F32), vmem((2, n_heads, 128), F32),
            vmem((g4, plane, 2, q_local, dim), BF16), vmem((g4, plane, 2, 128), F32), vmem((g4, n, n, 2, key_local, dim), BF16),
            vmem((g4, 2, n, n, n, 2, q_local, dim), BF16), vmem((g4, 2, n, n, n, 2, 128), F32),
            vmem((2, n, plane // unit_rows, 2, 128), F32),
            vmem((g4, n, n, 2, key_local, dim), BF16), vmem((g4, n, n, 2, key_local, dim), BF16), vmem((n * key_local, 128), jnp.int32),
            vmem((g4, n, n, 2, key_local, dim), F32), vmem((g4, n, n, 2, key_local, dim), F32), vmem((g4, n, n, 2, key_local, dim), F32),
            vmem((g4, 2, n, dim, block), F32), vmem((g4, n, dim, block), F32), vmem((g4, n - 1, dim, block), F32),
            vmem((g4, plane, q_local, dim), BF16), vmem((n_heads, q_local, dim), BF16),
            vmem((q_rows, dim), F32), vmem((k_rows, dim), F32), vmem((k_rows, dim), F32), vmem((q_rows, dim), BF16),
            dma((6,)), dma((g4,)), dma((g4,)), dma((g4,)), dma((g4,)), dma((g4,)), dma((g4,)), dma((g4,)), dma((g4,)), dma((2, g4)), dma((2, g4)),
            dma((g4,)), dma((g4,)),
            dma((g4, n)), dma((g4, n)), dma((g4, n)), dma((g4, n)), dma((g4, n)), dma((g4, n, n)), dma((g4,)), dma((g4,)), dma((g4,)), dma((g4,)), dma((g4,)), dma((g4,)),
            dma((3,)),
        ]
        anywhere = pl.BlockSpec(memory_space=pl.ANY)
        dq, dk, dv = pl.pallas_call(
            functools.partial(kernel, n, prefix0, dim ** -0.5, n_heads),
            name="exchange_and_backward",
            out_shape=(jax.ShapeDtypeStruct((q_rows, dim), BF16), jax.ShapeDtypeStruct((k_rows, dim), F32), jax.ShapeDtypeStruct((k_rows, dim), F32)),
            in_specs=[anywhere] * 6,
            out_specs=[anywhere] * 3,
            scratch_shapes=scratch,
            compiler_params=pltpu.CompilerParams(has_side_effects=True, collective_id=0, vmem_limit_bytes=60 * 1024 * 1024),
        )(queries.reshape(q_rows, dim), key_vecs.reshape(k_rows, dim), value_vecs.reshape(k_rows, dim), attn_out.reshape(q_rows, dim),
          log_sum_exp[0], grad_out.reshape(q_rows, dim))
        return dq.reshape(queries.shape), dk.reshape(key_vecs.shape), dv.reshape(value_vecs.shape)

    return jax.shard_map(per_device, mesh=mesh, in_specs=(spec_q, spec_kv, spec_kv, spec_q, spec_lse, spec_q), out_specs=(spec_q, spec_kv, spec_kv), check_vma=False)
```

time: 1840 us -> 131 us (0.07)
  waiting for transfers between devices: 869 us -> 0 us
  local copies, waits for them, and re-layouts: 470 us -> 5.34 us
  matrix products: 290 us -> 0 us
  Pallas kernels: 0 us -> 125 us
  other arithmetic: 101 us -> 0 us
  blocking collectives: 74.4 us -> 0 us
    reduce_scatter x1 -> x0, waiting for transfers between devices: 737 us -> none  [per_device(): dq_seg = lax.psum_scatter(parts_q, 'cp', scatter_dimension=0) * score_scale]
    dynamic_slice x640 -> x0, local copies, waits for them, and re-layouts: 345 us -> none  [per_device(): lax.scan(source_step, kv_acc, (q_all, do_all, lse_all, delta_all, q_starts))]
    dot_general x640 -> x0, matrix products: 290 us -> none  [the longest x128 68.4 us: tile_backward(): jnp.einsum('hqk,qhd->khd', weights.astype(jnp.bfloat16), do_tile, preferr...]
    all_gather x2 -> x0, waiting for transfers between devices: 130 us -> none  [the longest x1 102 us: per_device(): do_all = lax.all_gather(grad_out[seg_idx], 'cp')]
    pallas_call x0 -> x1, Pallas kernels: none -> 125 us  [per_device(): pl.pallas_call(functools.partial(kernel, n, prefix0, dim ** (-0.5), n_hea...]
    dynamic_update_slice x128 -> x0, local copies, waits for them, and re-layouts: 119 us -> none  [per_device(): lax.scan(source_step, kv_acc, (q_all, do_all, lse_all, delta_all, q_starts))]
    add x257 -> x0, other arithmetic: 88.5 us -> none  [the longest x128 88 us: tile_backward(): q_pos = q_start + jnp.arange(q_tile.shape[0])]
    all_gather x2 -> x0, blocking collectives: 74.4 us -> none  [the longest x1 39 us: per_device(): delta_all = lax.all_gather(row_delta[seg_idx], 'cp')]
  transfers between devices with their start and end apart: 3 -> 0, of which waited for: 3 -> 0; matrix products, arithmetic and copies ran while one was open for 0% -> 0% of each run, Pallas kernels for 0% -> 0%
where the time goes in v2:
time: 131 us
  Pallas kernels  125 us (95%)
  local copies, waits for them, and re-layouts  5.34 us (4%)
    pallas_call x1, Pallas kernels, per_device(): pl.pallas_call(functools.partial(kernel, n, prefix0, dim ** (-0.5), n_hea...  125 us
    unnamed x5, local copies, waits for them, and re-layouts  5.34 us

profile of v2, /device:TPU:0, one launch (start us, length us, event | category | flops | bytes accessed | tf_op | source)
XLA Modules:
  0.0 130.5 jit_solution(17940746692177453958)
XLA Ops:
  0.6 124.5 %exchange_and_backward.1 = (bf16[896,128]{1,0:T(8,128)(2,1)}, f32[2688,128]{1,0:T(8,128)}, f32[2688,128]{1,0:T(8,128)}) custom-call(bf16[896,128]{1,0:T(8,128)(2,1)} %bitcast.14, bf16[2688,128]{1,0:T(8,128)(2,1)} %bitcast.11, bf16[2688,128]{1,0:T(8,128)(2,1)} %bitcast.12, bf16[896,128]{1,0:T(8,128)(2,1)} %bitcast.15, f32[16,56]{1,0:T(8,128)} %bitcast.17, ...), custom_call_target="tpu_custom_call" | custom-call | tf_op jit(solution)/shard_map/exchange_and_backward/pallas_call | solution.py:502
  125.2 1.6 %copy.12 = bf16[1,16,56,128]{3,2,1,0:T(8,128)(2,1)} copy(bf16[1,16,56,128]{3,2,1,0:T(8,128)(2,1)} %bitcast.13) | data formatting | bytes 458752
  126.8 0.0 copy-start
  126.8 2.6 %copy.13 = f32[48,56,128]{2,1,0:T(8,128)} copy(f32[48,56,128]{2,1,0:T(8,128)} %bitcast.10) | data formatting | bytes 2752512
  129.4 0.0 copy-done
  129.4 1.1 copy.14
Async XLA Ops:
  126.8 2.6 %copy-start = (f32[2688,128]{1,0:T(8,128)S(1)}, f32[2688,128]{1,0:T(8,128)}, u32[]{:S(2)}) copy-start(f32[2688,128]{1,0:T(8,128)} %get-tuple-element.8) | copy-start | bytes 4128772

commit v3 on v2

--- a/solution.py
+++ b/solution.py
@@ -21,33 +21,34 @@
 def pick(table, g):
     if isinstance(g, int):
         return table[g]
-    value = table[-1]
-    for k in range(len(table) - 1):
-        value = jnp.where(g == k, table[k], value)
-    return value
+    return (sum(v << (4 * k) for k, v in enumerate(table)) >> (4 * g)) & 15
 
 
 def rank_at(n, a, b):
-    size = 8 if n == 4 else 4
-    pos = a * n + b
-    block, place = lax.div(pos, size), lax.rem(pos, size)
-    rank = lax.rem(place + 2 * size - 1 - block * 2, size)
-    return block * (size - 1) + rank, rank < size - 1
+    if n == 2:
+        rank = (a * 2 + b + 3) & 3
+        return rank, rank < 3
+    block = a >> 1
+    rank = (((a & 1) << 2) + b + 7 - 2 * block) & 7
+    return block * 7 + rank, rank < 7
 
 
 class Spot:
-    def __init__(self, n, coords, chip, core, g):
-        strides = (n * n, n, 1)
+    def __init__(self, n, chip, core, g):
+        bits = n // 2
         self.n, self.chip, self.core = n, chip, core
-        self.s_line, self.s_a, self.s_b = (pick([strides[t[k]] for k in range(GROUPS)], g) for t in (LINE_AXIS, FIRST_AXIS, SECOND_AXIS))
-        self.line, self.a, self.b = (pick([coords[t[k]] for k in range(GROUPS)], g) for t in (LINE_AXIS, FIRST_AXIS, SECOND_AXIS))
+        self.s_line, self.s_a, self.s_b = (pick([(2 - axis) * bits for axis in table], g) for table in (LINE_AXIS, FIRST_AXIS, SECOND_AXIS))
+        self.line, self.a, self.b = ((chip >> s) & (n - 1) for s in (self.s_line, self.s_a, self.s_b))
 
     def turn(self, c, d):
-        return lax.rem(c + d + self.n, self.n)
+        return (c + d) & (self.n - 1)
 
     def at(self, a=0, b=0, line=0):
-        return (self.chip + (self.turn(self.a, a) - self.a) * self.s_a + (self.turn(self.b, b) - self.b) * self.s_b
-                + (self.turn(self.line, line) - self.line) * self.s_line)
+        chip = self.chip
+        for c, d, s in ((self.a, a, self.s_a), (self.b, b, self.s_b), (self.line, line, self.s_line)):
+            if not (isinstance(d, int) and d == 0):
+                chip = chip + ((self.turn(c, d) - c) << s)
+        return chip
 
     def device(self, a=0, b=0, line=0):
         return (0, self.at(a, b, line) * 2 + self.core)
@@ -59,14 +60,14 @@
 def kernel(n, prefix0, scale, n_heads, q_in, k_in, v_in, o_in, lse_in, do_in, dq_out, dk_out, dv_out,
            q_raw, k_raw, v_raw, o_raw, lse_raw, do_raw, q_f32, do_f32, k_f32, v_f32, lse_pad, aux_rows,
            q_src, aux_src, kv_src, qd, aux, rows, kv1, kv2, kpos_buf, res, ret1, ret2, dqt, part, line_sum, dq_src, dq_got,
-           dq_f32, dk_f32, dv_f32, dq_bf,
+           dq_f32, dk_f32, dv_f32, dq_bf, p_buf, ds_buf,
            in_sem, q_send, q_recv, aux_send, aux_recv, ql_send, ql_recv, al_send, al_recv, pair_send, pair_recv, k1_send, k1_recv,
            k2_send, k2_recv, r1_send, r1_recv, r2_send, r2_recv, part_send, part_recv, ls_send, ls_recv, dq_send, dq_recv, out_sem):
     me = lax.axis_index("cp")
-    chip, core = lax.div(me, 2), lax.rem(me, 2)
-    coords = (lax.div(chip, n * n), lax.rem(lax.div(chip, n), n), lax.rem(chip, n))
+    chip, core = me >> 1, me & 1
+    bits = n // 2
     partner = (0, chip * 2 + 1 - core)
-    spots = [Spot(n, coords, chip, core, g) for g in range(GROUPS)]
+    spots = [Spot(n, chip, core, g) for g in range(GROUPS)]
     holds = [s.rank()[1] for s in spots]
     heads = n_heads // GROUPS
     q_local, key_local = q_src.shape[3], kv_src.shape[4]
@@ -115,7 +116,9 @@
     lse_t = lse_pad[...].T[0:n_heads]
     head_group = lax.div(lax.broadcasted_iota(jnp.int32, (n_heads, 128), 0), heads)
     lane = lax.broadcasted_iota(jnp.int32, (n_heads, 128), 1)
-    base = pick([lax.rem(s.b * n + s.a, unit_rows) * q_local for s in spots], head_group)
+    base = jnp.zeros((n_heads, 128), jnp.int32)
+    for g, spot in enumerate(spots):
+        base = jnp.where(head_group == g, ((spot.b * n + spot.a) & (unit_rows - 1)) * q_local, base)
     row_lse, row_delta = jnp.zeros((n_heads, 128), F32), jnp.zeros((n_heads, 128), F32)
     for t in range(q_local):
         at = pl.ds(t * n_heads, n_heads)
@@ -125,52 +128,43 @@
     aux_rows[0] = row_lse
     aux_rows[1] = row_delta
 
-    def lay_out_q(i, carry):
-        g = lax.div(i, plane)
-        spot = Spot(n, coords, chip, core, g)
-        rank, _ = spot.rank(lax.div(lax.rem(i, plane), n), lax.rem(i, n))
-        h = g * heads + lax.rem(rank, heads)
-        u = lax.rem(i, plane)
-        q_src[g, u, 0] = q_f32[pl.ds(h, q_local, stride=n_heads), :].astype(BF16)
-        q_src[g, u, 1] = do_f32[pl.ds(h, q_local, stride=n_heads), :].astype(BF16)
-        aux_src[g, u, 0:1] = aux_rows[0, pl.ds(h, 1), :]
-        aux_src[g, u, 1:2] = aux_rows[1, pl.ds(h, 1), :]
-        return carry
-
-    lax.fori_loop(0, GROUPS * plane, lay_out_q, 0)
+    for g, spot in enumerate(spots):
+        def lay_out_q(u, carry):
+            rank, _ = spot.rank(u >> bits, u & (n - 1))
+            h = g * heads + jnp.minimum(rank, heads - 1)
+            q_src[g, u, 0] = q_f32[pl.ds(h, q_local, stride=n_heads), :].astype(BF16)
+            q_src[g, u, 1] = do_f32[pl.ds(h, q_local, stride=n_heads), :].astype(BF16)
+            aux_src[g, u, 0:1] = aux_rows[0, pl.ds(h, 1), :]
+            aux_src[g, u, 1:2] = aux_rows[1, pl.ds(h, 1), :]
+            return carry
+
+        lax.fori_loop(0, plane, lay_out_q, 0, unroll=8)
     for copy in loads[4:]:
         copy.wait()
     widen(k_raw, k_f32, key_local)
     widen(v_raw, v_f32, key_local)
 
-    def lay_out_kv(i, carry):
-        g = lax.div(i, plane)
-        spot = Spot(n, coords, chip, core, g)
-        d1, d2 = lax.div(lax.rem(i, plane), n), lax.rem(i, n)
-        rank, _ = spot.rank(d1, d2)
-        h = g * heads + lax.rem(rank, heads)
-        kv_src[g, d1, d2, 0] = k_f32[pl.ds(h, key_local, stride=n_heads), :].astype(BF16)
-        kv_src[g, d1, d2, 1] = v_f32[pl.ds(h, key_local, stride=n_heads), :].astype(BF16)
-        return carry
-
-    lax.fori_loop(0, GROUPS * plane, lay_out_kv, 0)
+    for g, spot in enumerate(spots):
+        def lay_out_kv(u, carry):
+            rank, _ = spot.rank(u >> bits, u & (n - 1))
+            h = g * heads + jnp.minimum(rank, heads - 1)
+            kv_src[g, u >> bits, u & (n - 1), 0] = k_f32[pl.ds(h, key_local, stride=n_heads), :].astype(BF16)
+            kv_src[g, u >> bits, u & (n - 1), 1] = v_f32[pl.ds(h, key_local, stride=n_heads), :].astype(BF16)
+            return carry
+
+        lax.fori_loop(0, plane, lay_out_kv, 0, unroll=4)
     pl.semaphore_wait(barrier, met)
 
-    def send_q():
-        def go(i, carry):
-            g, u = lax.div(i, plane), lax.rem(i, plane)
-            spot = Spot(n, coords, chip, core, g)
-            d1, d2 = lax.div(u, n), lax.rem(u, n)
-
-            @pl.when(jnp.logical_and(u > 0, spot.rank(d1, d2)[1]))
+    def send_q(g):
+        spot = spots[g]
+        for u in range(1, plane):
+            d1, d2 = u >> bits, u & (n - 1)
+
+            @pl.when(spot.rank(d1, d2)[1])
             def _():
                 there = spot.device(d1, d2)
                 remote(q_src.at[g, u], qd.at[g, 0, spot.line, spot.b, spot.a], q_send.at[g], q_recv.at[g], there).start()
                 remote(aux_src.at[g, u], aux.at[g, 0, spot.line, spot.b, spot.a], aux_send.at[g], aux_recv.at[g], there).start()
-
-            return carry
-
-        lax.fori_loop(0, GROUPS * plane, go, 0)
 
     def k_first(g):
         for d in range(1, n):
@@ -192,12 +186,9 @@
             remote(qd.at[g, 0, spots[g].line], qd.at[g, 0, spots[g].line], ql_send.at[g], ql_recv.at[g], there).start()
             remote(aux.at[g, 0, spots[g].line], aux.at[g, 0, spots[g].line], al_send.at[g], al_recv.at[g], there).start()
 
-    send_q()
-    for g in range(GROUPS):
-        k_first(g)
-    for g in range(GROUPS):
-        k_second(g, True)
-    for g, spot in enumerate(spots):
+    def meet_plane(g):
+        spot = spots[g]
+
         @pl.when(holds[g])
         def _():
             qd[g, 0, spot.line, spot.b, spot.a] = q_src[g, 0]
@@ -207,6 +198,17 @@
             q_line(g)
 
     for g in range(GROUPS):
+        send_q(g)
+        if g < 2:
+            k_first(g)
+            k_second(g, True)
+    meet_plane(0)
+    for g in range(2, GROUPS):
+        k_first(g)
+        k_second(g, True)
+    for g in range(1, GROUPS):
+        meet_plane(g)
+    for g in range(GROUPS):
         wait_bytes(kv1.at[g, pl.ds(1, n - 1)], k1_recv.at[g])
         k_second(g, False)
 
@@ -227,14 +229,14 @@
     n_chunks = GROUPS * n
 
     def chunk_of(i):
-        g = lax.div(i, n)
-        return g, lax.rem(lax.rem(i, n) + jnp.where(g == GROUPS - 1, 1, 0), n)
+        g = i >> bits
+        return g, (i + jnp.where(g == GROUPS - 1, 1, 0)) & (n - 1)
 
     def compute(i):
         g, o2 = chunk_of(i)
-        spot = Spot(n, coords, chip, core, g)
-
-        @pl.when(lax.rem(i, n) == 0)
+        spot = Spot(n, chip, core, g)
+
+        @pl.when((i & (n - 1)) == 0)
         def _():
             for copy in pair_copies(g):
                 copy.wait()
@@ -260,31 +262,37 @@
         keys = kv2[g, o2, :, 0].reshape(keys_in, 128)
         values = kv2[g, o2, :, 1].reshape(keys_in, 128)
         keys_t = keys.T
-        res[g, o2] = jnp.zeros(res.shape[2:], F32)
 
         def q_step(s, carry):
-            half = lax.rem(s, 2)
-            l = spot.turn(spot.line, 1 + lax.div(s, 2))
+            half = s & 1
+            l = spot.turn(spot.line, 1 + (s >> 1))
             q = qd[g, half, l, :, :, 0].reshape(block, 128)
             do = qd[g, half, l, :, :, 1].reshape(block, 128)
             lse2 = jnp.concatenate([rows[half, l, r, 0:1, 0:width] for r in range(n_rows)], axis=1) * LOG2E
             delta = jnp.concatenate([rows[half, l, r, 1:2, 0:width] for r in range(n_rows)], axis=1)
             lanes = lax.broadcasted_iota(jnp.int32, (1, block), 1)
             unit = lax.div(lanes, q_local)
-            q_chip = l * spot.s_line + lax.div(unit, n) * spot.s_b + lax.rem(unit, n) * spot.s_a
-            qpos = (q_chip * 2 + lax.rem(core + half, 2)) * q_local + lax.rem(lanes, q_local)
+            q_chip = (l << spot.s_line) + (lax.div(unit, n) << spot.s_b) + (lax.rem(unit, n) << spot.s_a)
+            qpos = (q_chip * 2 + ((core + half) & 1)) * q_local + lax.rem(lanes, q_local)
             kpos = jnp.concatenate([kpos_buf[...]] * n_rows, axis=1)[:, 0:block]
             s_ = lax.dot_general(keys, q, (((1,), (1,)), ((), ())), preferred_element_type=F32)
             p = jnp.where(kpos <= qpos, jnp.exp2(s_ * (scale * LOG2E) - lse2), 0.0)
             dp = lax.dot_general(values, do, (((1,), (1,)), ((), ())), preferred_element_type=F32)
             ds = (p * (dp - delta)).astype(BF16)
-            res[g, o2, :, 0] += jnp.dot(ds, q, preferred_element_type=F32).reshape(n, key_local, 128)
-            res[g, o2, :, 1] += jnp.dot(p.astype(BF16), do, preferred_element_type=F32).reshape(n, key_local, 128)
-            dqt[g, half, l] += jnp.dot(keys_t, ds, preferred_element_type=F32)
+            at = pl.ds(pl.multiple_of((half * n + l) * block, block), block)
+            p_buf[:, at] = p.astype(BF16)
+            ds_buf[:, at] = ds
             return carry
 
-        lax.fori_loop(0, 2 * n, q_step, 0)
-        res[g, o2, :, 0] = res[g, o2, :, 0] * scale
+        lax.fori_loop(0, 2 * n, q_step, 0, unroll=8)
+        q_all = qd[g, :, :, :, :, 0].reshape(2 * n * block, 128)
+        do_all = qd[g, :, :, :, :, 1].reshape(2 * n * block, 128)
+        for half in range(2):
+            for l in range(n):
+                at = pl.ds((half * n + l) * block, block)
+                dqt[g, half, l] += jnp.dot(keys_t, ds_buf[:, at], preferred_element_type=F32)
+        res[g, o2, :, 0] = (jnp.dot(ds_buf[...], q_all, preferred_element_type=F32) * scale).reshape(n, key_local, 128)
+        res[g, o2, :, 1] = jnp.dot(p_buf[...], do_all, preferred_element_type=F32).reshape(n, key_local, 128)
 
     def part_copy(g):
         return remote(dqt.at[g, 1], part.at[g], part_send.at[g], part_recv.at[g], partner)
@@ -293,9 +301,9 @@
         return remote(dqt.at[g, 0, spot.turn(spot.line, d)], line_sum.at[g, n - 1 - d], ls_send.at[g], ls_recv.at[g], spot.device(line=d))
 
     def dq_copy(g, spot, u):
-        b, a = spot.turn(spot.b, lax.div(u, n)), spot.turn(spot.a, lax.rem(u, n))
-        h = g * heads + lax.rem(spot.rank()[0], heads)
-        return remote(dq_src.at[g, b * n + a], dq_got.at[h], dq_send.at[g], dq_recv.at[g], spot.device(a=lax.rem(u, n), b=lax.div(u, n)))
+        b, a = spot.turn(spot.b, u >> bits), spot.turn(spot.a, u & (n - 1))
+        h = g * heads + jnp.minimum(spot.rank()[0], heads - 1)
+        return remote(dq_src.at[g, b * n + a], dq_got.at[h], dq_send.at[g], dq_recv.at[g], spot.device(a=u & (n - 1), b=u >> bits))
 
     def first_back(g, o2, spot):
         return remote(res.at[g, o2], ret1.at[g, o2], r1_send.at[g, o2], r1_recv.at[g, o2], spot.device(b=-o2))
@@ -307,7 +315,7 @@
         @pl.when(i < n_chunks)
         def _():
             g, o2 = chunk_of(i)
-            spot = Spot(n, coords, chip, core, g)
+            spot = Spot(n, chip, core, g)
 
             @pl.when(spot.rank()[1])
             def _():
@@ -322,18 +330,18 @@
                     for o1 in range(1, n):
                         second_back(g, 0, o1, spot, res).start()
 
-        @pl.when(jnp.logical_and(lax.rem(i, n) == n - 1, i < n_chunks))
-        def _():
-            g = lax.div(i, n)
-
-            @pl.when(Spot(n, coords, chip, core, g).rank()[1])
+        @pl.when(jnp.logical_and((i & (n - 1)) == n - 1, i < n_chunks))
+        def _():
+            g = (i >> bits)
+
+            @pl.when(Spot(n, chip, core, g).rank()[1])
             def _():
                 part_copy(g).start()
 
-        @pl.when(jnp.logical_and(lax.rem(i, n) == 0, jnp.logical_and(i >= n, i <= n_chunks)))
-        def _():
-            g = lax.div(i, n) - 1
-            spot = Spot(n, coords, chip, core, g)
+        @pl.when(jnp.logical_and((i & (n - 1)) == 0, jnp.logical_and(i >= n, i <= n_chunks)))
+        def _():
+            g = (i >> bits) - 1
+            spot = Spot(n, chip, core, g)
 
             @pl.when(spot.rank()[1])
             def _():
@@ -343,10 +351,10 @@
                 for d in range(1, n):
                     line_copy(g, spot, d).start()
 
-        @pl.when(jnp.logical_and(lax.rem(i, n) == 1, jnp.logical_and(i >= n, i <= n_chunks + 1)))
-        def _():
-            g = lax.div(i, n) - 1
-            spot = Spot(n, coords, chip, core, g)
+        @pl.when(jnp.logical_and((i & (n - 1)) == 1, jnp.logical_and(i >= n, i <= n_chunks + 1)))
+        def _():
+            g = (i >> bits) - 1
+            spot = Spot(n, chip, core, g)
 
             @pl.when(spot.rank()[1])
             def _():
@@ -364,11 +372,11 @@
 
                 lax.fori_loop(1, plane, go, 0)
 
-        @pl.when(jnp.logical_and(lax.rem(i, n) == n - 2, i < n_chunks - n))
-        def _():
-            g = lax.div(i, n) + 1
-
-            @pl.when(Spot(n, coords, chip, core, g).rank()[1])
+        @pl.when(jnp.logical_and((i & (n - 1)) == n - 2, i < n_chunks - n))
+        def _():
+            g = (i >> bits) + 1
+
+            @pl.when(Spot(n, chip, core, g).rank()[1])
             def _():
                 share_queries(g)
 
@@ -377,7 +385,7 @@
         @pl.when(jnp.logical_and(j >= 0, j < n_chunks))
         def _():
             g, o2 = chunk_of(j)
-            spot = Spot(n, coords, chip, core, g)
+            spot = Spot(n, chip, core, g)
 
             @pl.when(jnp.logical_and(o2 > 0, spot.rank(b=o2)[1]))
             def _():
@@ -390,7 +398,7 @@
         @pl.when(k >= 0)
         def _():
             g, o2 = chunk_of(k)
-            spot = Spot(n, coords, chip, core, g)
+            spot = Spot(n, chip, core, g)
 
             def put(o1, src):
                 rank, _ = spot.rank(a=o1, b=o2)
@@ -493,6 +501,7 @@
             vmem((g4, 2, n, dim, block), F32), vmem((g4, n, dim, block), F32), vmem((g4, n - 1, dim, block), F32),
             vmem((g4, plane, q_local, dim), BF16), vmem((n_heads, q_local, dim), BF16),
             vmem((q_rows, dim), F32), vmem((k_rows, dim), F32), vmem((k_rows, dim), F32), vmem((q_rows, dim), BF16),
+            vmem((n * key_local, 2 * n * block), BF16), vmem((n * key_local, 2 * n * block), BF16),
             dma((6,)), dma((g4,)), dma((g4,)), dma((g4,)), dma((g4,)), dma((g4,)), dma((g4,)), dma((g4,)), dma((g4,)), dma((2, g4)), dma((2, g4)),
             dma((g4,)), dma((g4,)),
             dma((g4, n)), dma((g4, n)), dma((g4, n)), dma((g4, n)), dma((g4, n)), dma((g4, n, n)), dma((g4,)), dma((g4,)), dma((g4,)), dma((g4,)), dma((g4,)), dma((g4,)),

time: 131 us -> 108 us (0.82)
  Pallas kernels: 125 us -> 102 us
    pallas_call x1, Pallas kernels: 125 us -> 102 us  [per_device(): pl.pallas_call(functools.partial(kernel, n, prefix0, dim ** (-0.5), n_hea...]
where the time goes in v3:
time: 108 us
  Pallas kernels  102 us (94%)
  local copies, waits for them, and re-layouts  5.34 us (5%)
    pallas_call x1, Pallas kernels, per_device(): pl.pallas_call(functools.partial(kernel, n, prefix0, dim ** (-0.5), n_hea...  102 us
    unnamed x5, local copies, waits for them, and re-layouts  5.34 us

profile of v3, /device:TPU:0, one launch (start us, length us, event | category | flops | bytes accessed | tf_op | source)
XLA Modules:
  0.0 107.5 jit_solution(17612313740452034265)
XLA Ops:
  0.6 101.5 %exchange_and_backward.1 = (bf16[896,128]{1,0:T(8,128)(2,1)}, f32[2688,128]{1,0:T(8,128)}, f32[2688,128]{1,0:T(8,128)}) custom-call(bf16[896,128]{1,0:T(8,128)(2,1)} %bitcast.14, bf16[2688,128]{1,0:T(8,128)(2,1)} %bitcast.11, bf16[2688,128]{1,0:T(8,128)(2,1)} %bitcast.12, bf16[896,128]{1,0:T(8,128)(2,1)} %bitcast.15, f32[16,56]{1,0:T(8,128)} %bitcast.17, ...), custom_call_target="tpu_custom_call" | custom-call | tf_op jit(solution)/shard_map/exchange_and_backward/pallas_call | solution.py:511
  102.2 1.6 %copy.12 = bf16[1,16,56,128]{3,2,1,0:T(8,128)(2,1)} copy(bf16[1,16,56,128]{3,2,1,0:T(8,128)(2,1)} %bitcast.13) | data formatting | bytes 458752
  103.8 0.0 copy-start
  103.8 2.6 %copy.13 = f32[48,56,128]{2,1,0:T(8,128)} copy(f32[48,56,128]{2,1,0:T(8,128)} %bitcast.10) | data formatting | bytes 2752512
  106.4 0.0 copy-done
  106.4 1.1 %copy.14 = f32[48,56,128]{2,1,0:T(8,128)} copy(f32[48,56,128]{2,1,0:T(8,128)S(1)} %bitcast.9) | data formatting | bytes 2752512
Async XLA Ops:
  103.8 2.6 %copy-start = (f32[2688,128]{1,0:T(8,128)S(1)}, f32[2688,128]{1,0:T(8,128)}, u32[]{:S(2)}) copy-start(f32[2688,128]{1,0:T(8,128)} %get-tuple-element.8) | copy-start | bytes 4128772

commit v4 on v3

--- a/solution.py
+++ b/solution.py
@@ -9,12 +9,16 @@
 
 MESH = pl.DeviceIdType.MESH
 GROUPS = 4
-LINE_AXIS = (0, 1, 2, 0)
-FIRST_AXIS = (1, 2, 0, 2)
-SECOND_AXIS = (2, 0, 1, 1)
+LINE_AXIS, FIRST_AXIS, SECOND_AXIS = zip((1, 0, 2), (2, 1, 0), (0, 2, 1), (0, 1, 2))
+CHUNKS = ((3, 1), (3, 3), (3, 0), (3, 2), (2, 2), (0, 1), (0, 3), (0, 0), (1, 0), (1, 1), (1, 3), (0, 2), (2, 3), (2, 1), (1, 2), (2, 0))
+BEFORE = (("q1", 3), ("q1", 1), ("q1", 2), ("q1", 0), ("k1", 3), ("k1", 0), ("q2", 3), ("q2", 1), ("q2", 0), ("k1", 2), ("k2", 0), ("line", 3),
+          ("q2", 2), ("line", 0), ("k2", 3), ("line", 2), ("k1", 1), ("line", 1), ("k2", 2))
+AFTER = {2: (("k2", 1),)}
 LOG2E = 1.4426950408889634
-FORWARD_LAG = 2
-STORE_LAG = 4
+FORWARD_LAG = 6
+SUM_LAG = 7
+STORE_LAG = 16
+VMEM_MIB = 46
 F32, BF16 = jnp.float32, jnp.bfloat16
 
 
@@ -57,12 +61,12 @@
         return rank_at(self.n, self.turn(self.a, a), self.turn(self.b, b))
 
 
-def kernel(n, prefix0, scale, n_heads, q_in, k_in, v_in, o_in, lse_in, do_in, dq_out, dk_out, dv_out,
-           q_raw, k_raw, v_raw, o_raw, lse_raw, do_raw, q_f32, do_f32, k_f32, v_f32, lse_pad, aux_rows,
-           q_src, aux_src, kv_src, qd, aux, rows, kv1, kv2, kpos_buf, res, ret1, ret2, dqt, part, line_sum, dq_src, dq_got,
-           dq_f32, dk_f32, dv_f32, dq_bf, p_buf, ds_buf,
-           in_sem, q_send, q_recv, aux_send, aux_recv, ql_send, ql_recv, al_send, al_recv, pair_send, pair_recv, k1_send, k1_recv,
-           k2_send, k2_recv, r1_send, r1_recv, r2_send, r2_recv, part_send, part_recv, ls_send, ls_recv, dq_send, dq_recv, out_sem):
+def kernel(n, prefix0, scale, n_heads, q_raw, k_raw, v_raw, o_raw, lse_raw, do_raw, dq_bf, dk_f32, dv_f32,
+           q_f32, do_f32, k_f32, v_f32, lse_pad, aux_rows,
+           q_src, aux_src, kv_src, q1, qd, aux, rows, kv1, kv2, kpos_buf, res, ret1, ret2, dqt, part, line_sum, dq_src, dq_got,
+           dq_f32, p_buf, ds_buf,
+           q1_send, q1_recv, q2_send, q2_recv, aux_send, aux_recv, ql_send, ql_recv, al_send, al_recv, pair_send, pair_recv, k1_send, k1_recv,
+           k2_send, k2_recv, r1_send, r1_recv, r2_send, r2_recv, part_send, part_recv, ls_send, ls_recv, dq_send, dq_recv):
     me = lax.axis_index("cp")
     chip, core = me >> 1, me & 1
     bits = n // 2
@@ -70,7 +74,7 @@
     spots = [Spot(n, chip, core, g) for g in range(GROUPS)]
     holds = [s.rank()[1] for s in spots]
     heads = n_heads // GROUPS
-    q_local, key_local = q_src.shape[3], kv_src.shape[4]
+    q_local, key_local = q_src.shape[4], kv_src.shape[4]
     plane = n * n
     unit_rows = min(8, plane)
     width = unit_rows * q_local
@@ -83,11 +87,6 @@
 
     def wait_bytes(ref, sem):
         pltpu.make_async_copy(ref, ref, sem).wait()
-
-    loads = [pltpu.make_async_copy(a, b, in_sem.at[k]) for k, (a, b) in enumerate(
-        [(q_in, q_raw), (do_in, do_raw), (o_in, o_raw), (lse_in, lse_raw), (k_in, k_raw), (v_in, v_raw)])]
-    for copy in loads:
-        copy.start()
 
     barrier = pltpu.get_barrier_semaphore()
     met = 1
@@ -108,8 +107,6 @@
 
         lax.fori_loop(0, count // 4, go, 0)
 
-    for copy in loads[:4]:
-        copy.wait()
     widen(q_raw, q_f32, q_local)
     widen(do_raw, do_f32, q_local)
     lse_pad[0:q_local, 0:n_heads] = lse_raw[...]
@@ -132,15 +129,13 @@
         def lay_out_q(u, carry):
             rank, _ = spot.rank(u >> bits, u & (n - 1))
             h = g * heads + jnp.minimum(rank, heads - 1)
-            q_src[g, u, 0] = q_f32[pl.ds(h, q_local, stride=n_heads), :].astype(BF16)
-            q_src[g, u, 1] = do_f32[pl.ds(h, q_local, stride=n_heads), :].astype(BF16)
+            q_src[g, u >> bits, u & (n - 1), 0] = q_f32[pl.ds(h, q_local, stride=n_heads), :].astype(BF16)
+            q_src[g, u >> bits, u & (n - 1), 1] = do_f32[pl.ds(h, q_local, stride=n_heads), :].astype(BF16)
             aux_src[g, u, 0:1] = aux_rows[0, pl.ds(h, 1), :]
             aux_src[g, u, 1:2] = aux_rows[1, pl.ds(h, 1), :]
             return carry
 
         lax.fori_loop(0, plane, lay_out_q, 0, unroll=8)
-    for copy in loads[4:]:
-        copy.wait()
     widen(k_raw, k_f32, key_local)
     widen(v_raw, v_f32, key_local)
 
@@ -155,16 +150,34 @@
         lax.fori_loop(0, plane, lay_out_kv, 0, unroll=4)
     pl.semaphore_wait(barrier, met)
 
-    def send_q(g):
+    def q_first(g):
         spot = spots[g]
+        for d in range(1, n):
+            remote(q_src.at[g, d], q1.at[g, d], q1_send.at[g], q1_recv.at[g], spot.device(a=d)).start()
         for u in range(1, plane):
             d1, d2 = u >> bits, u & (n - 1)
 
             @pl.when(spot.rank(d1, d2)[1])
             def _():
-                there = spot.device(d1, d2)
-                remote(q_src.at[g, u], qd.at[g, 0, spot.line, spot.b, spot.a], q_send.at[g], q_recv.at[g], there).start()
-                remote(aux_src.at[g, u], aux.at[g, 0, spot.line, spot.b, spot.a], aux_send.at[g], aux_recv.at[g], there).start()
+                remote(aux_src.at[g, u], aux.at[g, 0, spot.line, spot.b, spot.a], aux_send.at[g], aux_recv.at[g], spot.device(d1, d2)).start()
+
+    def q_second(g):
+        spot = spots[g]
+        wait_bytes(q1.at[g, pl.ds(1, n - 1)], q1_recv.at[g])
+
+        @pl.when(holds[g])
+        def _():
+            for o1 in range(n):
+                qd[g, 0, spot.line, spot.b, spot.turn(spot.a, -o1)] = q1[g, o1, 0] if o1 else q_src[g, 0, 0]
+            aux[g, 0, spot.line, spot.b, spot.a] = aux_src[g, 0]
+
+        for d in range(1, n):
+            @pl.when(spot.rank(b=d)[1])
+            def _():
+                there = spot.device(b=d)
+                for o1 in range(n):
+                    src = q1.at[g, o1, d] if o1 else q_src.at[g, 0, d]
+                    remote(src, qd.at[g, 0, spot.line, spot.b, spot.turn(spot.a, -o1)], q2_send.at[g, d], q2_recv.at[g], there).start()
 
     def k_first(g):
         for d in range(1, n):
@@ -186,31 +199,20 @@
             remote(qd.at[g, 0, spots[g].line], qd.at[g, 0, spots[g].line], ql_send.at[g], ql_recv.at[g], there).start()
             remote(aux.at[g, 0, spots[g].line], aux.at[g, 0, spots[g].line], al_send.at[g], al_recv.at[g], there).start()
 
-    def meet_plane(g):
-        spot = spots[g]
-
+    def line_out(g):
         @pl.when(holds[g])
         def _():
-            qd[g, 0, spot.line, spot.b, spot.a] = q_src[g, 0]
-            aux[g, 0, spot.line, spot.b, spot.a] = aux_src[g, 0]
-            wait_bytes(q_src.at[g, pl.ds(1, plane - 1)], q_recv.at[g])
+            wait_bytes(q_src.at[g, pl.ds(1, n - 1)], q2_recv.at[g])
             wait_bytes(aux_src.at[g, pl.ds(1, plane - 1)], aux_recv.at[g])
             q_line(g)
 
-    for g in range(GROUPS):
-        send_q(g)
-        if g < 2:
-            k_first(g)
-            k_second(g, True)
-    meet_plane(0)
-    for g in range(2, GROUPS):
+    def pass_on(g):
+        wait_bytes(kv1.at[g, pl.ds(1, n - 1)], k1_recv.at[g])
+        k_second(g, False)
+
+    def keys_out(g):
         k_first(g)
         k_second(g, True)
-    for g in range(1, GROUPS):
-        meet_plane(g)
-    for g in range(GROUPS):
-        wait_bytes(kv1.at[g, pl.ds(1, n - 1)], k1_recv.at[g])
-        k_second(g, False)
 
     def pair_copies(g):
         return (remote(qd.at[g, 0], qd.at[g, 1], pair_send.at[0, g], pair_recv.at[0, g], partner),
@@ -222,28 +224,44 @@
         for copy in pair_copies(g):
             copy.start()
 
-    @pl.when(holds[0])
-    def _():
-        share_queries(0)
-
-    n_chunks = GROUPS * n
+    acts = {"q1": q_first, "q2": q_second, "k1": keys_out, "k2": pass_on, "line": line_out}
+    chunks = [(g, o2) for g, o2 in CHUNKS if o2 < n]
+    n_chunks = len(chunks)
+    first = [min(k for k, c in enumerate(chunks) if c[0] == g) for g in range(GROUPS)]
+    last = [max(k for k, c in enumerate(chunks) if c[0] == g) for g in range(GROUPS)]
+    after = {k: list(v) for k, v in AFTER.items()} if n == 4 else {-1: [a for v in AFTER.values() for a in v]}
+    lined = {g: k for k, v in after.items() for name, g in v if name == "line"}
+    for name, g in list(BEFORE) + after.pop(-1, []):
+        acts[name](g)
+    shares = {g: max(first[g] - 2, lined.get(g, -1), -1) for g in range(GROUPS)}
+
+    def share(g):
+        pl.when(holds[g])(lambda: share_queries(g))
+
+    for g in range(GROUPS):
+        if shares[g] < 0:
+            share(g)
+    codes = [sum((g * 4 + o2) << (4 * k) for k, (g, o2) in enumerate(chunks[w:w + 8])) for w in range(0, n_chunks, 8)]
+    codes = [c - (1 << 32) if c >= 1 << 31 else c for c in codes]
+    begins = sum(1 << k for k in first)
 
     def chunk_of(i):
-        g = i >> bits
-        return g, (i + jnp.where(g == GROUPS - 1, 1, 0)) & (n - 1)
+        word = codes[0] if len(codes) == 1 else jnp.where(i < 8, codes[0], codes[1])
+        code = word >> (4 * (i & 7))
+        return (code >> 2) & 3, code & 3
 
     def compute(i):
         g, o2 = chunk_of(i)
         spot = Spot(n, chip, core, g)
 
-        @pl.when((i & (n - 1)) == 0)
+        @pl.when(((begins >> i) & 1) == 1)
         def _():
             for copy in pair_copies(g):
                 copy.wait()
             for half in range(2):
                 for l in range(n):
                     units = aux[g, half, l].reshape(n_rows, unit_rows, 2, 128)
-                    rows[half, l] = jnp.sum(units, axis=1)
+                    rows[g, half, l] = jnp.sum(units, axis=1)
             dqt[g] = jnp.zeros(dqt.shape[1:], F32)
 
         @pl.when(o2 == 0)
@@ -268,8 +286,8 @@
             l = spot.turn(spot.line, 1 + (s >> 1))
             q = qd[g, half, l, :, :, 0].reshape(block, 128)
             do = qd[g, half, l, :, :, 1].reshape(block, 128)
-            lse2 = jnp.concatenate([rows[half, l, r, 0:1, 0:width] for r in range(n_rows)], axis=1) * LOG2E
-            delta = jnp.concatenate([rows[half, l, r, 1:2, 0:width] for r in range(n_rows)], axis=1)
+            lse2 = jnp.concatenate([rows[g, half, l, r, 0:1, 0:width] for r in range(n_rows)], axis=1) * LOG2E
+            delta = jnp.concatenate([rows[g, half, l, r, 1:2, 0:width] for r in range(n_rows)], axis=1)
             lanes = lax.broadcasted_iota(jnp.int32, (1, block), 1)
             unit = lax.div(lanes, q_local)
             q_chip = (l << spot.s_line) + (lax.div(unit, n) << spot.s_b) + (lax.rem(unit, n) << spot.s_a)
@@ -330,20 +348,18 @@
                     for o1 in range(1, n):
                         second_back(g, 0, o1, spot, res).start()
 
-        @pl.when(jnp.logical_and((i & (n - 1)) == n - 1, i < n_chunks))
-        def _():
-            g = (i >> bits)
-
-            @pl.when(Spot(n, chip, core, g).rank()[1])
+        for k, todo in after.items():
+            @pl.when(i == k)
+            def _():
+                for name, g in todo:
+                    acts[name](g)
+
+        for g, spot in enumerate(spots):
+            @pl.when(jnp.logical_and(i == last[g], holds[g]))
             def _():
                 part_copy(g).start()
 
-        @pl.when(jnp.logical_and((i & (n - 1)) == 0, jnp.logical_and(i >= n, i <= n_chunks)))
-        def _():
-            g = (i >> bits) - 1
-            spot = Spot(n, chip, core, g)
-
-            @pl.when(spot.rank()[1])
+            @pl.when(jnp.logical_and(i == last[g] + 1, holds[g]))
             def _():
                 part_copy(g).wait()
                 for l in range(n):
@@ -351,12 +367,7 @@
                 for d in range(1, n):
                     line_copy(g, spot, d).start()
 
-        @pl.when(jnp.logical_and((i & (n - 1)) == 1, jnp.logical_and(i >= n, i <= n_chunks + 1)))
-        def _():
-            g = (i >> bits) - 1
-            spot = Spot(n, chip, core, g)
-
-            @pl.when(spot.rank()[1])
+            @pl.when(jnp.logical_and(i == last[g] + 1 + SUM_LAG, holds[g]))
             def _():
                 wait_bytes(line_sum.at[g], ls_recv.at[g])
                 total = dqt[g, 0, spot.line]
@@ -372,13 +383,10 @@
 
                 lax.fori_loop(1, plane, go, 0)
 
-        @pl.when(jnp.logical_and((i & (n - 1)) == n - 2, i < n_chunks - n))
-        def _():
-            g = (i >> bits) + 1
-
-            @pl.when(Spot(n, chip, core, g).rank()[1])
-            def _():
-                share_queries(g)
+            if shares[g] >= 0:
+                @pl.when(i == shares[g])
+                def _():
+                    share(g)
 
         j = i - FORWARD_LAG
 
@@ -395,7 +403,7 @@
 
         k = i - STORE_LAG
 
-        @pl.when(k >= 0)
+        @pl.when(jnp.logical_and(k >= 0, k < n_chunks))
         def _():
             g, o2 = chunk_of(k)
             spot = Spot(n, chip, core, g)
@@ -422,11 +430,8 @@
 
         return carry
 
-    lax.fori_loop(0, n_chunks + STORE_LAG, step, 0)
-
-    outs = [pltpu.make_async_copy(dk_f32, dk_out, out_sem.at[0]), pltpu.make_async_copy(dv_f32, dv_out, out_sem.at[1])]
-    for copy in outs:
-        copy.start()
+    lax.fori_loop(0, n_chunks + max(STORE_LAG, SUM_LAG + 2), step, 0)
+
     for g in range(GROUPS):
         for mine in (False, True):
             @pl.when(holds[g] if mine else jnp.logical_not(holds[g]))
@@ -439,16 +444,14 @@
 
     lax.fori_loop(0, n_heads, put_dq, 0)
     dq_bf[...] = dq_f32[...].astype(BF16)
-    dq_copy_out = pltpu.make_async_copy(dq_bf, dq_out, out_sem.at[2])
-    dq_copy_out.start()
 
     for g, spot in enumerate(spots):
         for mine in (False, True):
             @pl.when(holds[g] if mine else jnp.logical_not(holds[g]))
             def _():
-                wait_bytes(q_src.at[g, pl.ds(0, heads - mine)], q_send.at[g])
                 wait_bytes(aux_src.at[g, pl.ds(0, heads - mine)], aux_send.at[g])
         wait_bytes(kv1.at[g, pl.ds(1, n - 1)], k1_send.at[g])
+        wait_bytes(q1.at[g, pl.ds(1, n - 1)], q1_send.at[g])
 
         @pl.when(holds[g])
         def _():
@@ -464,11 +467,17 @@
             @pl.when(spot.rank(b=d)[1])
             def _():
                 wait_bytes(kv2.at[g, d], k2_send.at[g, d])
+                wait_bytes(q1.at[g, d], q2_send.at[g, d])
                 wait_bytes(res.at[g, d, pl.ds(1, n - 1)], r2_send.at[g, d])
 
-    for copy in outs:
+
+def write_out(*refs):
+    count = len(refs) // 2
+    copies = [pltpu.make_async_copy(refs[k], refs[count + k], refs[-1].at[k]) for k in range(count)]
+    for copy in copies:
+        copy.start()
+    for copy in copies:
         copy.wait()
-    dq_copy_out.wait()
 
 
 def solution(mesh):
@@ -489,35 +498,44 @@
         g4 = GROUPS
         vmem = pltpu.VMEM
         scratch = [
-            vmem((q_rows, dim), BF16), vmem((k_rows, dim), BF16), vmem((k_rows, dim), BF16), vmem((q_rows, dim), BF16),
-            vmem((q_local, n_heads), F32), vmem((q_rows, dim), BF16),
             vmem((q_rows, dim), F32), vmem((q_rows, dim), F32), vmem((k_rows, dim), F32), vmem((k_rows, dim), F32),
             vmem((128, 128), F32), vmem((2, n_heads, 128), F32),
-            vmem((g4, plane, 2, q_local, dim), BF16), vmem((g4, plane, 2, 128), F32), vmem((g4, n, n, 2, key_local, dim), BF16),
+            vmem((g4, n, n, 2, q_local, dim), BF16), vmem((g4, plane, 2, 128), F32), vmem((g4, n, n, 2, key_local, dim), BF16),
+            vmem((g4, n, n, 2, q_local, dim), BF16),
             vmem((g4, 2, n, n, n, 2, q_local, dim), BF16), vmem((g4, 2, n, n, n, 2, 128), F32),
-            vmem((2, n, plane // unit_rows, 2, 128), F32),
+            vmem((g4, 2, n, plane // unit_rows, 2, 128), F32),
             vmem((g4, n, n, 2, key_local, dim), BF16), vmem((g4, n, n, 2, key_local, dim), BF16), vmem((n * key_local, 128), jnp.int32),
             vmem((g4, n, n, 2, key_local, dim), F32), vmem((g4, n, n, 2, key_local, dim), F32), vmem((g4, n, n, 2, key_local, dim), F32),
             vmem((g4, 2, n, dim, block), F32), vmem((g4, n, dim, block), F32), vmem((g4, n - 1, dim, block), F32),
             vmem((g4, plane, q_local, dim), BF16), vmem((n_heads, q_local, dim), BF16),
-            vmem((q_rows, dim), F32), vmem((k_rows, dim), F32), vmem((k_rows, dim), F32), vmem((q_rows, dim), BF16),
+            vmem((q_rows, dim), F32),
             vmem((n * key_local, 2 * n * block), BF16), vmem((n * key_local, 2 * n * block), BF16),
-            dma((6,)), dma((g4,)), dma((g4,)), dma((g4,)), dma((g4,)), dma((g4,)), dma((g4,)), dma((g4,)), dma((g4,)), dma((2, g4)), dma((2, g4)),
+            dma((g4,)), dma((g4,)), dma((g4, n)), dma((g4,)), dma((g4,)), dma((g4,)), dma((g4,)), dma((g4,)), dma((g4,)), dma((g4,)), dma((2, g4)), dma((2, g4)),
             dma((g4,)), dma((g4,)),
             dma((g4, n)), dma((g4, n)), dma((g4, n)), dma((g4, n)), dma((g4, n)), dma((g4, n, n)), dma((g4,)), dma((g4,)), dma((g4,)), dma((g4,)), dma((g4,)), dma((g4,)),
-            dma((3,)),
         ]
         anywhere = pl.BlockSpec(memory_space=pl.ANY)
-        dq, dk, dv = pl.pallas_call(
+        shapes = (jax.ShapeDtypeStruct((q_rows, dim), BF16), jax.ShapeDtypeStruct((k_rows, dim), F32), jax.ShapeDtypeStruct((k_rows, dim), F32))
+        inside = pl.BlockSpec(memory_space=pltpu.VMEM)
+        results = pl.pallas_call(
             functools.partial(kernel, n, prefix0, dim ** -0.5, n_heads),
             name="exchange_and_backward",
-            out_shape=(jax.ShapeDtypeStruct((q_rows, dim), BF16), jax.ShapeDtypeStruct((k_rows, dim), F32), jax.ShapeDtypeStruct((k_rows, dim), F32)),
-            in_specs=[anywhere] * 6,
-            out_specs=[anywhere] * 3,
+            out_shape=shapes,
+            in_specs=[inside] * 6,
+            out_specs=[inside] * 3,
             scratch_shapes=scratch,
-            compiler_params=pltpu.CompilerParams(has_side_effects=True, collective_id=0, vmem_limit_bytes=60 * 1024 * 1024),
+            compiler_params=pltpu.CompilerParams(has_side_effects=True, collective_id=0, vmem_limit_bytes=VMEM_MIB * 1024 * 1024),
         )(queries.reshape(q_rows, dim), key_vecs.reshape(k_rows, dim), value_vecs.reshape(k_rows, dim), attn_out.reshape(q_rows, dim),
           log_sum_exp[0], grad_out.reshape(q_rows, dim))
+        dq, dk, dv = pl.pallas_call(
+            write_out,
+            name="write_out",
+            out_shape=shapes,
+            in_specs=[inside] * 3,
+            out_specs=[anywhere] * 3,
+            scratch_shapes=[dma((3,))],
+            compiler_params=pltpu.CompilerParams(vmem_limit_bytes=8 * 1024 * 1024),
+        )(*results)
         return dq.reshape(queries.shape), dk.reshape(key_vecs.shape), dv.reshape(value_vecs.shape)
 
     return jax.shard_map(per_device, mesh=mesh, in_specs=(spec_q, spec_kv, spec_kv, spec_q, spec_lse, spec_q), out_specs=(spec_q, spec_kv, spec_kv), check_vma=False)

time: 108 us -> 85.5 us (0.79)
  Pallas kernels: 102 us -> 78.9 us
    pallas_call x1, Pallas kernels: 102 us -> 77.2 us  [per_device(): pl.pallas_call(functools.partial(kernel, n, prefix0, dim ** (-0.5), n_hea...]
    pallas_call x0 -> x1, Pallas kernels: none -> 1.64 us  [per_device(): pl.pallas_call(write_out, name='write_out', out_shape=shapes, in_specs=[i...]
    unnamed x5 -> x12, local copies, waits for them, and re-layouts: 5.34 us -> 5.7 us
where the time goes in v4:
time: 85.5 us; the launch traced here: 85.2 us
  Pallas kernels  78.9 us (92%)
  local copies, waits for them, and re-layouts  5.7 us (7%)
    pallas_call x1, Pallas kernels, per_device(): pl.pallas_call(functools.partial(kernel, n, prefix0, dim ** (-0.5), n_hea...  77.2 us
    unnamed x12, local copies, waits for them, and re-layouts  5.7 us

profile of v4, /device:TPU:0, one launch (start us, length us, event | category | flops | bytes accessed | tf_op | source)
XLA Modules:
  0.0 85.2 jit_solution(4190077934533342976)
XLA Ops:
  0.6 0.0 copy-start
  0.6 1.1 %copy-done = bf16[48,56,128]{2,1,0:T(8,128)(2,1)S(1)} copy-done((bf16[48,56,128]{2,1,0:T(8,128)(2,1)S(1)}, bf16[48,56,128]{2,1,0:T(8,128)(2,1)}, u32[]{:S(2)}) %copy-start) | copy-done | bytes 688152
  1.7 0.0 copy-start.1
  1.7 1.1 %copy-done.1 = bf16[48,56,128]{2,1,0:T(8,128)(2,1)S(1)} copy-done((bf16[48,56,128]{2,1,0:T(8,128)(2,1)S(1)}, bf16[48,56,128]{2,1,0:T(8,128)(2,1)}, u32[]{:S(2)}) %copy-start.1) | copy-done | bytes 688152
  2.8 0.0 copy-start.2
  2.8 0.9 %copy-done.2 = bf16[1,16,56,128]{3,2,1,0:T(8,128)(2,1)S(1)} copy-done((bf16[1,16,56,128]{3,2,1,0:T(8,128)(2,1)S(1)}, bf16[1,16,56,128]{3,2,1,0:T(8,128)(2,1)}, u32[]{:S(2)}) %copy-start.2) | copy-done | bytes 229400
  3.8 0.0 copy-start.3
  3.8 0.9 %copy-done.3 = bf16[1,16,56,128]{3,2,1,0:T(8,128)(2,1)S(1)} copy-done((bf16[1,16,56,128]{3,2,1,0:T(8,128)(2,1)S(1)}, bf16[1,16,56,128]{3,2,1,0:T(8,128)(2,1)}, u32[]{:S(2)}) %copy-start.3) | copy-done | bytes 229400
  4.7 0.0 copy-start.4
  4.7 0.9 %copy-done.4 = bf16[1,16,56,128]{3,2,1,0:T(8,128)(2,1)S(1)} copy-done((bf16[1,16,56,128]{3,2,1,0:T(8,128)(2,1)S(1)}, bf16[1,16,56,128]{3,2,1,0:T(8,128)(2,1)}, u32[]{:S(2)}) %copy-start.4) | copy-done | bytes 229400
  5.6 0.0 copy-start.5
  5.7 0.7 copy-done.5
  6.3 77.2 %exchange_and_backward.1 = (bf16[896,128]{1,0:T(8,128)(2,1)S(1)}, f32[2688,128]{1,0:T(8,128)S(1)}, f32[2688,128]{1,0:T(8,128)S(1)}) custom-call(bf16[896,128]{1,0:T(8,128)(2,1)S(1)} %bitcast.11, bf16[2688,128]{1,0:T(8,128)(2,1)S(1)} %bitcast.9, bf16[2688,128]{1,0:T(8,128)(2,1)S(1)} %bitcast.10, bf16[896,128]{1,0:T(8,128)(2,1)S(1)} %bitcast.12, ...), custom_call_target="tpu_custom_call" | custom-call | tf_op jit(solution)/shard_map/exchange_and_backward/pallas_call | solution.py:520
  83.6 1.6 %write_out.1 = (bf16[896,128]{1,0:T(8,128)(2,1)}, f32[2688,128]{1,0:T(8,128)}, f32[2688,128]{1,0:T(8,128)}) custom-call(bf16[896,128]{1,0:T(8,128)(2,1)S(1)} %get-tuple-element.9.refs_0_, f32[2688,128]{1,0:T(8,128)S(1)} %get-tuple-element.10.refs_1_, f32[2688,128]{1,0:T(8,128)S(1)} %get-tuple-element.11.refs_2_), custom_call_target="tpu_custom_call" | custom-call | tf_op jit(solution)/shard_map/write_out/pallas_call | solution.py:530
Async XLA Ops:
  0.6 1.1 %copy-start = (bf16[48,56,128]{2,1,0:T(8,128)(2,1)S(1)}, bf16[48,56,128]{2,1,0:T(8,128)(2,1)}, u32[]{:S(2)}) copy-start(bf16[48,56,128]{2,1,0:T(8,128)(2,1)} %param.7) | copy-start | bytes 2064388
  1.7 1.1 %copy-start.1 = (bf16[48,56,128]{2,1,0:T(8,128)(2,1)S(1)}, bf16[48,56,128]{2,1,0:T(8,128)(2,1)}, u32[]{:S(2)}) copy-start(bf16[48,56,128]{2,1,0:T(8,128)(2,1)} %param.8) | copy-start | bytes 2064388
  2.8 0.9 %copy-start.2 = (bf16[1,16,56,128]{3,2,1,0:T(8,128)(2,1)S(1)}, bf16[1,16,56,128]{3,2,1,0:T(8,128)(2,1)}, u32[]{:S(2)}) copy-start(bf16[1,16,56,128]{3,2,1,0:T(8,128)(2,1)} %param.6) | copy-start | bytes 688132
  3.8 0.9 %copy-start.3 = (bf16[1,16,56,128]{3,2,1,0:T(8,128)(2,1)S(1)}, bf16[1,16,56,128]{3,2,1,0:T(8,128)(2,1)}, u32[]{:S(2)}) copy-start(bf16[1,16,56,128]{3,2,1,0:T(8,128)(2,1)} %param.9) | copy-start | bytes 688132
  4.7 0.9 %copy-start.4 = (bf16[1,16,56,128]{3,2,1,0:T(8,128)(2,1)S(1)}, bf16[1,16,56,128]{3,2,1,0:T(8,128)(2,1)}, u32[]{:S(2)}) copy-start(bf16[1,16,56,128]{3,2,1,0:T(8,128)(2,1)} %param.11) | copy-start | bytes 688132
  5.6 0.7 copy-start.5

commit v5 on v4

--- a/solution.py
+++ b/solution.py
@@ -9,15 +9,16 @@
 
 MESH = pl.DeviceIdType.MESH
 GROUPS = 4
-LINE_AXIS, FIRST_AXIS, SECOND_AXIS = zip((1, 0, 2), (2, 1, 0), (0, 2, 1), (0, 1, 2))
-CHUNKS = ((3, 1), (3, 3), (3, 0), (3, 2), (2, 2), (0, 1), (0, 3), (0, 0), (1, 0), (1, 1), (1, 3), (0, 2), (2, 3), (2, 1), (1, 2), (2, 0))
-BEFORE = (("q1", 3), ("q1", 1), ("q1", 2), ("q1", 0), ("k1", 3), ("k1", 0), ("q2", 3), ("q2", 1), ("q2", 0), ("k1", 2), ("k2", 0), ("line", 3),
-          ("q2", 2), ("line", 0), ("k2", 3), ("line", 2), ("k1", 1), ("line", 1), ("k2", 2))
-AFTER = {2: (("k2", 1),)}
+LINE_AXIS, FIRST_AXIS, SECOND_AXIS = zip((2, 1, 0), (0, 1, 2), (1, 0, 2), (1, 2, 0))
+CHUNKS = ((0, 3), (0, 1), (1, 2), (2, 0), (2, 2), (0, 2), (0, 0), (3, 2), (2, 3), (3, 0), (3, 3), (3, 1), (2, 1), (1, 3), (1, 0), (1, 1))
+BEFORE = (("k1", 0), ("q1", 0), ("k1", 1), ("q2", 0), ("q2", 2), ("q2", 3), ("k1", 2), ("q1", 1), ("q2", 1), ("line", 0), ("line", 1), ("k2", 0),
+          ("line", 2), ("q1", 3), ("line", 3), ("k1", 3), ("line2", 0), ("line2", 2), ("line2", 1), ("q1", 2), ("k2", 1), ("k2", 2), ("k2", 3))
+AFTER = {0: (("line2", 3),)}
 LOG2E = 1.4426950408889634
 FORWARD_LAG = 6
-SUM_LAG = 7
-STORE_LAG = 16
+RELAY_LAG = 3
+SUM_LAG = 14
+STORE_LAG = 20
 VMEM_MIB = 46
 F32, BF16 = jnp.float32, jnp.bfloat16
 
@@ -61,12 +62,12 @@
         return rank_at(self.n, self.turn(self.a, a), self.turn(self.b, b))
 
 
-def kernel(n, prefix0, scale, n_heads, q_raw, k_raw, v_raw, o_raw, lse_raw, do_raw, dq_bf, dk_f32, dv_f32,
-           q_f32, do_f32, k_f32, v_f32, lse_pad, aux_rows,
-           q_src, aux_src, kv_src, q1, qd, aux, rows, kv1, kv2, kpos_buf, res, ret1, ret2, dqt, part, line_sum, dq_src, dq_got,
+def kernel(n, prefix0, scale, n_heads, q_in, k_in, v_in, o_in, lse_in, do_in, dq_bf, dk_f32, dv_f32,
+           q_raw, k_raw, v_raw, o_raw, lse_raw, do_raw, q_f32, do_f32, k_f32, v_f32, lse_pad, aux_rows,
+           q_src, aux_src, kv_src, q1, qd, aux, rows, kv1, kv2, kpos_buf, res, ret1, ret2, dqt, part, line_half, line_sum, dq_src, dq_got,
            dq_f32, p_buf, ds_buf,
-           q1_send, q1_recv, q2_send, q2_recv, aux_send, aux_recv, ql_send, ql_recv, al_send, al_recv, pair_send, pair_recv, k1_send, k1_recv,
-           k2_send, k2_recv, r1_send, r1_recv, r2_send, r2_recv, part_send, part_recv, ls_send, ls_recv, dq_send, dq_recv):
+           in_sem, q1_send, q1_recv, q2_send, q2_recv, aux_send, aux_recv, ql_send, ql_recv, ql2_send, ql2_recv, al_send, al_recv, pair_send, pair_recv, k1_send, k1_recv,
+           k2_send, k2_recv, r1_send, r1_recv, r2_send, r2_recv, part_send, part_recv, lh_send, lh_recv, ls_send, ls_recv, dq_send, dq_recv):
     me = lax.axis_index("cp")
     chip, core = me >> 1, me & 1
     bits = n // 2
@@ -88,13 +89,20 @@
     def wait_bytes(ref, sem):
         pltpu.make_async_copy(ref, ref, sem).wait()
 
+    loads = [pltpu.make_async_copy(a, b, in_sem.at[k]) for k, (a, b) in enumerate(
+        [(q_in, q_raw), (do_in, do_raw), (o_in, o_raw), (lse_in, lse_raw), (k_in, k_raw), (v_in, v_raw)])]
+    for copy in loads:
+        copy.start()
+
     barrier = pltpu.get_barrier_semaphore()
     met = 1
     pl.semaphore_signal(barrier, inc=1, device_id=partner, device_id_type=MESH)
-    for g, spot in enumerate(spots[:3]):
+    for s_a, s_b in ((2 * bits, bits), (bits, 0), (0, 2 * bits)):
+        c_a, c_b = (chip >> s_a) & (n - 1), (chip >> s_b) & (n - 1)
         for a in range(n):
             for b in range(1, n):
-                pl.semaphore_signal(barrier, inc=1, device_id=spot.device(a, b), device_id_type=MESH)
+                there = chip + ((((c_a + a) & (n - 1)) - c_a) << s_a) + ((((c_b + b) & (n - 1)) - c_b) << s_b)
+                pl.semaphore_signal(barrier, inc=1, device_id=(0, there * 2 + core), device_id_type=MESH)
                 met += 1
 
     def widen(src, dst, count):
@@ -107,8 +115,127 @@
 
         lax.fori_loop(0, count // 4, go, 0)
 
+    order = [g for name, g in BEFORE if name == "q1"]
+    for copy in loads[:2]:
+        copy.wait()
     widen(q_raw, q_f32, q_local)
     widen(do_raw, do_f32, q_local)
+    for g in order:
+        spot = spots[g]
+
+        def lay_out_q(u, carry):
+            rank, _ = spot.rank(u >> bits, u & (n - 1))
+            h = g * heads + jnp.minimum(rank, heads - 1)
+            q_src[g, u >> bits, u & (n - 1), 0] = q_f32[pl.ds(h, q_local, stride=n_heads), :].astype(BF16)
+            q_src[g, u >> bits, u & (n - 1), 1] = do_f32[pl.ds(h, q_local, stride=n_heads), :].astype(BF16)
+            return carry
+
+        lax.fori_loop(0, plane, lay_out_q, 0, unroll=8)
+    pl.semaphore_wait(barrier, met)
+
+    def q_first(g):
+        spot = spots[g]
+        for d in range(1, n):
+            remote(q_src.at[g, d], q1.at[g, d], q1_send, q1_recv.at[g], spot.device(a=d)).start()
+
+    def aux_out(g):
+        spot = spots[g]
+        for u in range(1, plane):
+            d1, d2 = u >> bits, u & (n - 1)
+
+            @pl.when(spot.rank(d1, d2)[1])
+            def _():
+                remote(aux_src.at[g, u], aux.at[g, 0, spot.line, spot.b, spot.a], aux_send.at[g], aux_recv.at[g], spot.device(d1, d2)).start()
+
+    def q_second(g):
+        spot = spots[g]
+        wait_bytes(q1.at[g, pl.ds(1, n - 1)], q1_recv.at[g])
+
+        @pl.when(holds[g])
+        def _():
+            for o1 in range(n):
+                qd[g, 0, spot.line, spot.b, spot.turn(spot.a, -o1)] = q1[g, o1, 0] if o1 else q_src[g, 0, 0]
+            aux[g, 0, spot.line, spot.b, spot.a] = aux_src[g, 0]
+
+        for d in range(1, n):
+            @pl.when(spot.rank(b=d)[1])
+            def _():
+                there = spot.device(b=d)
+                for o1 in range(n):
+                    src = q1.at[g, o1, d] if o1 else q_src.at[g, 0, d]
+                    remote(src, qd.at[g, 0, spot.line, spot.b, spot.turn(spot.a, -o1)], q2_send.at[g], q2_recv.at[g], there).start()
+
+    def k_first(g):
+        for d in range(1, n):
+            remote(kv_src.at[g, d], kv1.at[g, d], k1_send, k1_recv.at[g], spots[g].device(a=d)).start()
+
+    def k_second(g, own):
+        for d in range(1, n):
+            @pl.when(spots[g].rank(b=d)[1])
+            def _():
+                there = spots[g].device(b=d)
+                if own:
+                    remote(kv_src.at[g, 0, d], kv2.at[g, d, 0], k2_send.at[g], k2_recv.at[g, d - 1], there).start()
+                else:
+                    remote(kv1.at[g, pl.ds(1, n - 1), d], kv2.at[g, d, pl.ds(1, n - 1)], k2_send.at[g], k2_recv.at[g, d - 1], there).start()
+
+    beside = (1, n - 1) if n == 4 else (1,)
+    n_half = n // 2
+
+    def q_line(g):
+        spot = spots[g]
+        for d in beside:
+            remote(qd.at[g, 0, spot.line], qd.at[g, 0, spot.line], ql_send.at[g], ql_recv.at[g], spot.device(line=d)).start()
+        for d in range(1, n):
+            remote(aux.at[g, 0, spot.line], aux.at[g, 0, spot.line], al_send.at[g], al_recv.at[g], spot.device(line=d)).start()
+
+    def line_on(g):
+        spot = spots[g]
+        if n == 4:
+            @pl.when(holds[g])
+            def _():
+                wait_bytes(qd.at[g, 0, pl.ds(0, 2)], ql_recv.at[g])
+                for k, (d, there) in enumerate(((n - 1, 1), (1, n - 1))):
+                    piece = qd.at[g, 0, spot.turn(spot.line, d), pl.ds(k * n_half, n_half)]
+                    remote(piece, piece, ql2_send.at[g], ql2_recv.at[g], spot.device(line=there)).start()
+
+    def line_out(g):
+        @pl.when(holds[g])
+        def _():
+            wait_bytes(q_src.at[g, pl.ds(1, n - 1)], q2_recv.at[g])
+            wait_bytes(aux_src.at[g, pl.ds(1, plane - 1)], aux_recv.at[g])
+            q_line(g)
+
+    def pass_on(g):
+        wait_bytes(kv1.at[g, pl.ds(1, n - 1)], k1_recv.at[g])
+        k_second(g, False)
+
+    def keys_out(g):
+        k_first(g)
+        k_second(g, True)
+
+    def pair_copies(g):
+        return (remote(qd.at[g, 0], qd.at[g, 1], pair_send.at[0, g], pair_recv.at[0, g], partner),
+                remote(aux.at[g, 0], aux.at[g, 1], pair_send.at[1, g], pair_recv.at[1, g], partner))
+
+    def share_queries(g):
+        wait_bytes(qd.at[g, 0, 0], ql2_recv.at[g] if n == 4 else ql_recv.at[g])
+        wait_bytes(aux.at[g, 0, pl.ds(0, n - 1)], al_recv.at[g])
+        for copy in pair_copies(g):
+            copy.start()
+
+    acts = {"q1": q_first, "q2": q_second, "k1": keys_out, "k2": pass_on, "line": line_out, "line2": line_on}
+    chunks = [(g, o2) for g, o2 in CHUNKS if o2 < n]
+    n_chunks = len(chunks)
+    first = [min(k for k, c in enumerate(chunks) if c[0] == g) for g in range(GROUPS)]
+    last = [max(k for k, c in enumerate(chunks) if c[0] == g) for g in range(GROUPS)]
+    after = {k: list(v) for k, v in AFTER.items()} if n == 4 else {-1: [a for v in AFTER.values() for a in v]}
+    lined = {g: k for k, v in after.items() for name, g in v if name == "line2"}
+    before = list(BEFORE) + after.pop(-1, [])
+    for g in order:
+        q_first(g)
+    for copy in loads[2:4]:
+        copy.wait()
     lse_pad[0:q_local, 0:n_heads] = lse_raw[...]
     lse_t = lse_pad[...].T[0:n_heads]
     head_group = lax.div(lax.broadcasted_iota(jnp.int32, (n_heads, 128), 0), heads)
@@ -124,22 +251,26 @@
         row_lse = jnp.where(lane == base + t, lse_t[:, t:t + 1], row_lse)
     aux_rows[0] = row_lse
     aux_rows[1] = row_delta
-
-    for g, spot in enumerate(spots):
-        def lay_out_q(u, carry):
+    for g in order:
+        spot = spots[g]
+
+        def lay_out_aux(u, carry):
             rank, _ = spot.rank(u >> bits, u & (n - 1))
             h = g * heads + jnp.minimum(rank, heads - 1)
-            q_src[g, u >> bits, u & (n - 1), 0] = q_f32[pl.ds(h, q_local, stride=n_heads), :].astype(BF16)
-            q_src[g, u >> bits, u & (n - 1), 1] = do_f32[pl.ds(h, q_local, stride=n_heads), :].astype(BF16)
             aux_src[g, u, 0:1] = aux_rows[0, pl.ds(h, 1), :]
             aux_src[g, u, 1:2] = aux_rows[1, pl.ds(h, 1), :]
             return carry
 
-        lax.fori_loop(0, plane, lay_out_q, 0, unroll=8)
+        lax.fori_loop(0, plane, lay_out_aux, 0, unroll=8)
+    for g in order:
+        aux_out(g)
+    for copy in loads[4:]:
+        copy.wait()
     widen(k_raw, k_f32, key_local)
     widen(v_raw, v_f32, key_local)
-
-    for g, spot in enumerate(spots):
+    for g in [g for name, g in before if name == "k1"]:
+        spot = spots[g]
+
         def lay_out_kv(u, carry):
             rank, _ = spot.rank(u >> bits, u & (n - 1))
             h = g * heads + jnp.minimum(rank, heads - 1)
@@ -148,91 +279,9 @@
             return carry
 
         lax.fori_loop(0, plane, lay_out_kv, 0, unroll=4)
-    pl.semaphore_wait(barrier, met)
-
-    def q_first(g):
-        spot = spots[g]
-        for d in range(1, n):
-            remote(q_src.at[g, d], q1.at[g, d], q1_send.at[g], q1_recv.at[g], spot.device(a=d)).start()
-        for u in range(1, plane):
-            d1, d2 = u >> bits, u & (n - 1)
-
-            @pl.when(spot.rank(d1, d2)[1])
-            def _():
-                remote(aux_src.at[g, u], aux.at[g, 0, spot.line, spot.b, spot.a], aux_send.at[g], aux_recv.at[g], spot.device(d1, d2)).start()
-
-    def q_second(g):
-        spot = spots[g]
-        wait_bytes(q1.at[g, pl.ds(1, n - 1)], q1_recv.at[g])
-
-        @pl.when(holds[g])
-        def _():
-            for o1 in range(n):
-                qd[g, 0, spot.line, spot.b, spot.turn(spot.a, -o1)] = q1[g, o1, 0] if o1 else q_src[g, 0, 0]
-            aux[g, 0, spot.line, spot.b, spot.a] = aux_src[g, 0]
-
-        for d in range(1, n):
-            @pl.when(spot.rank(b=d)[1])
-            def _():
-                there = spot.device(b=d)
-                for o1 in range(n):
-                    src = q1.at[g, o1, d] if o1 else q_src.at[g, 0, d]
-                    remote(src, qd.at[g, 0, spot.line, spot.b, spot.turn(spot.a, -o1)], q2_send.at[g, d], q2_recv.at[g], there).start()
-
-    def k_first(g):
-        for d in range(1, n):
-            remote(kv_src.at[g, d], kv1.at[g, d], k1_send.at[g], k1_recv.at[g], spots[g].device(a=d)).start()
-
-    def k_second(g, own):
-        for d in range(1, n):
-            @pl.when(spots[g].rank(b=d)[1])
-            def _():
-                there = spots[g].device(b=d)
-                if own:
-                    remote(kv_src.at[g, 0, d], kv2.at[g, d, 0], k2_send.at[g, d], k2_recv.at[g, d], there).start()
-                else:
-                    remote(kv1.at[g, pl.ds(1, n - 1), d], kv2.at[g, d, pl.ds(1, n - 1)], k2_send.at[g, d], k2_recv.at[g, d], there).start()
-
-    def q_line(g):
-        for d in range(1, n):
-            there = spots[g].device(line=d)
-            remote(qd.at[g, 0, spots[g].line], qd.at[g, 0, spots[g].line], ql_send.at[g], ql_recv.at[g], there).start()
-            remote(aux.at[g, 0, spots[g].line], aux.at[g, 0, spots[g].line], al_send.at[g], al_recv.at[g], there).start()
-
-    def line_out(g):
-        @pl.when(holds[g])
-        def _():
-            wait_bytes(q_src.at[g, pl.ds(1, n - 1)], q2_recv.at[g])
-            wait_bytes(aux_src.at[g, pl.ds(1, plane - 1)], aux_recv.at[g])
-            q_line(g)
-
-    def pass_on(g):
-        wait_bytes(kv1.at[g, pl.ds(1, n - 1)], k1_recv.at[g])
-        k_second(g, False)
-
-    def keys_out(g):
-        k_first(g)
-        k_second(g, True)
-
-    def pair_copies(g):
-        return (remote(qd.at[g, 0], qd.at[g, 1], pair_send.at[0, g], pair_recv.at[0, g], partner),
-                remote(aux.at[g, 0], aux.at[g, 1], pair_send.at[1, g], pair_recv.at[1, g], partner))
-
-    def share_queries(g):
-        wait_bytes(qd.at[g, 0, pl.ds(0, n - 1)], ql_recv.at[g])
-        wait_bytes(aux.at[g, 0, pl.ds(0, n - 1)], al_recv.at[g])
-        for copy in pair_copies(g):
-            copy.start()
-
-    acts = {"q1": q_first, "q2": q_second, "k1": keys_out, "k2": pass_on, "line": line_out}
-    chunks = [(g, o2) for g, o2 in CHUNKS if o2 < n]
-    n_chunks = len(chunks)
-    first = [min(k for k, c in enumerate(chunks) if c[0] == g) for g in range(GROUPS)]
-    last = [max(k for k, c in enumerate(chunks) if c[0] == g) for g in range(GROUPS)]
-    after = {k: list(v) for k, v in AFTER.items()} if n == 4 else {-1: [a for v in AFTER.values() for a in v]}
-    lined = {g: k for k, v in after.items() for name, g in v if name == "line"}
-    for name, g in list(BEFORE) + after.pop(-1, []):
-        acts[name](g)
+    for name, g in before:
+        if name != "q1":
+            acts[name](g)
     shares = {g: max(first[g] - 2, lined.get(g, -1), -1) for g in range(GROUPS)}
 
     def share(g):
@@ -272,7 +321,7 @@
 
         @pl.when(o2 > 0)
         def _():
-            wait_bytes(kv2.at[g, o2], k2_recv.at[g, o2])
+            wait_bytes(kv2.at[g, o2], k2_recv.at[g, o2 - 1])
 
         for o1 in range(n):
             first = (spot.at(a=-o1, b=-o2) * 2 + core) * key_local - prefix0
@@ -315,8 +364,20 @@
     def part_copy(g):
         return remote(dqt.at[g, 1], part.at[g], part_send.at[g], part_recv.at[g], partner)
 
-    def line_copy(g, spot, d):
-        return remote(dqt.at[g, 0, spot.turn(spot.line, d)], line_sum.at[g, n - 1 - d], ls_send.at[g], ls_recv.at[g], spot.device(line=d))
+    def half_out(g, spot):
+        if n == 4:
+            for k, d in enumerate(beside):
+                src = dqt.at[g, 0, spot.turn(spot.line, 2), pl.ds(k * 64, 64)]
+                remote(src, line_half.at[g, k], lh_send.at[g], lh_recv.at[g], spot.device(line=d)).start()
+
+    def line_sum_out(g, spot):
+        if n == 4:
+            wait_bytes(line_half.at[g], lh_recv.at[g])
+            for k, d in enumerate(beside):
+                l = spot.turn(spot.line, d)
+                dqt[g, 0, l, k * 64:k * 64 + 64] = dqt[g, 0, l, k * 64:k * 64 + 64] + line_half[g, k]
+        for k, d in enumerate(beside):
+            remote(dqt.at[g, 0, spot.turn(spot.line, d)], line_sum.at[g, k], ls_send.at[g], ls_recv.at[g], spot.device(line=d)).start()
 
     def dq_copy(g, spot, u):
         b, a = spot.turn(spot.b, u >> bits), spot.turn(spot.a, u & (n - 1))
@@ -324,10 +385,10 @@
         return remote(dq_src.at[g, b * n + a], dq_got.at[h], dq_send.at[g], dq_recv.at[g], spot.device(a=u & (n - 1), b=u >> bits))
 
     def first_back(g, o2, spot):
-        return remote(res.at[g, o2], ret1.at[g, o2], r1_send.at[g, o2], r1_recv.at[g, o2], spot.device(b=-o2))
+        return remote(res.at[g, o2], ret1.at[g, o2], r1_send.at[g], r1_recv.at[g, o2 - 1], spot.device(b=-o2))
 
     def second_back(g, o2, o1, spot, src):
-        return remote(src.at[g, o2, o1], ret2.at[g, o2, o1], r2_send.at[g, o2], r2_recv.at[g, o2, o1], spot.device(a=-o1))
+        return remote(src.at[g, o2, o1], ret2.at[g, o2, o1], r2_send.at[g], r2_recv.at[g, o2], spot.device(a=-o1))
 
     def step(i, carry):
         @pl.when(i < n_chunks)
@@ -362,16 +423,20 @@
             @pl.when(jnp.logical_and(i == last[g] + 1, holds[g]))
             def _():
                 part_copy(g).wait()
-                for l in range(n):
+                for d in ((2, 1, 3, 0) if n == 4 else (1, 0)):
+                    l = spot.turn(spot.line, d)
                     dqt[g, 0, l] = dqt[g, 0, l] + part[g, l]
-                for d in range(1, n):
-                    line_copy(g, spot, d).start()
+                half_out(g, spot)
+
+            @pl.when(jnp.logical_and(i == last[g] + 1 + RELAY_LAG, holds[g]))
+            def _():
+                line_sum_out(g, spot)
 
             @pl.when(jnp.logical_and(i == last[g] + 1 + SUM_LAG, holds[g]))
             def _():
                 wait_bytes(line_sum.at[g], ls_recv.at[g])
                 total = dqt[g, 0, spot.line]
-                for d in range(n - 1):
+                for d in range(len(beside)):
                     total = total + line_sum[g, d]
                 dq_src[g] = (total * scale).T.astype(BF16).reshape(plane, q_local, 128)
                 h = g * heads + spot.rank()[0]
@@ -397,7 +462,7 @@
 
             @pl.when(jnp.logical_and(o2 > 0, spot.rank(b=o2)[1]))
             def _():
-                wait_bytes(ret1.at[g, o2], r1_recv.at[g, o2])
+                wait_bytes(ret1.at[g, o2], r1_recv.at[g, o2 - 1])
                 for o1 in range(1, n):
                     second_back(g, o2, o1, spot, ret1).start()
 
@@ -414,14 +479,18 @@
                 dk_f32[at, :] = src[g, o2, o1, 0]
                 dv_f32[at, :] = src[g, o2, o1, 1]
 
-            for o1 in range(n):
-                @pl.when(spot.rank(a=o1, b=o2)[1])
-                def _():
-                    if o1:
-                        wait_bytes(ret2.at[g, o2, o1], r2_recv.at[g, o2, o1])
-                        return
-                    pl.when(o2 == 0)(lambda: put(0, res))
-                    pl.when(o2 > 0)(lambda: put(0, ret1))
+            @pl.when(spot.rank(b=o2)[1])
+            def _():
+                pl.when(o2 == 0)(lambda: put(0, res))
+                pl.when(o2 > 0)(lambda: put(0, ret1))
+
+            column = spot.turn(spot.b, o2)
+            short = jnp.logical_and((column & 1) == 0, column != spot.a)
+            for less in range(2):
+                if n - 1 > less:
+                    @pl.when(short if less else jnp.logical_not(short))
+                    def _():
+                        wait_bytes(ret2.at[g, o2, pl.ds(1, n - 1 - less)], r2_recv.at[g, o2])
 
             for o1 in range(1, n):
                 @pl.when(spot.rank(a=o1, b=o2)[1])
@@ -445,30 +514,36 @@
     lax.fori_loop(0, n_heads, put_dq, 0)
     dq_bf[...] = dq_f32[...].astype(BF16)
 
+    wait_bytes(q1.at[pl.ds(0, GROUPS), pl.ds(1, n - 1)], q1_send)
+    wait_bytes(kv1.at[pl.ds(0, GROUPS), pl.ds(1, n - 1)], k1_send)
     for g, spot in enumerate(spots):
+        even = (spot.a & 1) == 0
         for mine in (False, True):
             @pl.when(holds[g] if mine else jnp.logical_not(holds[g]))
             def _():
                 wait_bytes(aux_src.at[g, pl.ds(0, heads - mine)], aux_send.at[g])
-        wait_bytes(kv1.at[g, pl.ds(1, n - 1)], k1_send.at[g])
-        wait_bytes(q1.at[g, pl.ds(1, n - 1)], q1_send.at[g])
+        short = jnp.logical_and(even, holds[g])
+        for less in range(2):
+            if n - 1 > less:
+                @pl.when(short if less else jnp.logical_not(short))
+                def _():
+                    wait_bytes(q1.at[g, pl.ds(0, n - 1 - less)], q2_send.at[g])
+                    wait_bytes(kv2.at[g, pl.ds(0, n - 1 - less)], k2_send.at[g])
+
+            @pl.when(even if less else jnp.logical_not(even))
+            def _():
+                wait_bytes(ret2.at[g, pl.ds(0, n - less), pl.ds(1, n - 1)], r2_send.at[g])
 
         @pl.when(holds[g])
         def _():
-            wait_bytes(qd.at[g, 0, pl.ds(0, n - 1)], ql_send.at[g])
+            wait_bytes(qd.at[g, 0, pl.ds(0, len(beside))], ql_send.at[g])
             wait_bytes(aux.at[g, 0, pl.ds(0, n - 1)], al_send.at[g])
             wait_bytes(line_sum.at[g], ls_send.at[g])
             wait_bytes(dq_src.at[g, pl.ds(1, plane - 1)], dq_send.at[g])
-            wait_bytes(res.at[g, 0, pl.ds(1, n - 1)], r2_send.at[g, 0])
-            for d in range(1, n):
-                wait_bytes(res.at[g, d], r1_send.at[g, d])
-
-        for d in range(1, n):
-            @pl.when(spot.rank(b=d)[1])
-            def _():
-                wait_bytes(kv2.at[g, d], k2_send.at[g, d])
-                wait_bytes(q1.at[g, d], q2_send.at[g, d])
-                wait_bytes(res.at[g, d, pl.ds(1, n - 1)], r2_send.at[g, d])
+            wait_bytes(ret1.at[g, pl.ds(0, n - 1)], r1_send.at[g])
+            if n == 4:
+                wait_bytes(qd.at[g, 0, 0], ql2_send.at[g])
+                wait_bytes(line_half.at[g], lh_send.at[g])
 
 
 def write_out(*refs):
@@ -498,6 +573,8 @@
         g4 = GROUPS
         vmem = pltpu.VMEM
         scratch = [
+            vmem((q_rows, dim), BF16), vmem((k_rows, dim), BF16), vmem((k_rows, dim), BF16), vmem((q_rows, dim), BF16),
+            vmem((q_local, n_heads), F32), vmem((q_rows, dim), BF16),
             vmem((q_rows, dim), F32), vmem((q_rows, dim), F32), vmem((k_rows, dim), F32), vmem((k_rows, dim), F32),
             vmem((128, 128), F32), vmem((2, n_heads, 128), F32),
             vmem((g4, n, n, 2, q_local, dim), BF16), vmem((g4, plane, 2, 128), F32), vmem((g4, n, n, 2, key_local, dim), BF16),
@@ -506,27 +583,28 @@
             vmem((g4, 2, n, plane // unit_rows, 2, 128), F32),
             vmem((g4, n, n, 2, key_local, dim), BF16), vmem((g4, n, n, 2, key_local, dim), BF16), vmem((n * key_local, 128), jnp.int32),
             vmem((g4, n, n, 2, key_local, dim), F32), vmem((g4, n, n, 2, key_local, dim), F32), vmem((g4, n, n, 2, key_local, dim), F32),
-            vmem((g4, 2, n, dim, block), F32), vmem((g4, n, dim, block), F32), vmem((g4, n - 1, dim, block), F32),
+            vmem((g4, 2, n, dim, block), F32), vmem((g4, n, dim, block), F32), vmem((g4, 2, dim // 2, block), F32), vmem((g4, n // 2, dim, block), F32),
             vmem((g4, plane, q_local, dim), BF16), vmem((n_heads, q_local, dim), BF16),
             vmem((q_rows, dim), F32),
             vmem((n * key_local, 2 * n * block), BF16), vmem((n * key_local, 2 * n * block), BF16),
-            dma((g4,)), dma((g4,)), dma((g4, n)), dma((g4,)), dma((g4,)), dma((g4,)), dma((g4,)), dma((g4,)), dma((g4,)), dma((g4,)), dma((2, g4)), dma((2, g4)),
-            dma((g4,)), dma((g4,)),
-            dma((g4, n)), dma((g4, n)), dma((g4, n)), dma((g4, n)), dma((g4, n)), dma((g4, n, n)), dma((g4,)), dma((g4,)), dma((g4,)), dma((g4,)), dma((g4,)), dma((g4,)),
+            dma((6,)), dma, dma((g4,)), dma((g4,)), dma((g4,)), dma((g4,)), dma((g4,)), dma((g4,)), dma((g4,)), dma((g4,)), dma((g4,)),
+            dma((g4,)), dma((g4,)), dma((2, g4)), dma((2, g4)), dma, dma((g4,)), dma((g4,)), dma((g4, n - 1)), dma((g4,)), dma((g4, n - 1)),
+            dma((g4,)), dma((g4, n)), dma((g4,)), dma((g4,)), dma((g4,)), dma((g4,)), dma((g4,)), dma((g4,)), dma((g4,)), dma((g4,)),
         ]
         anywhere = pl.BlockSpec(memory_space=pl.ANY)
         shapes = (jax.ShapeDtypeStruct((q_rows, dim), BF16), jax.ShapeDtypeStruct((k_rows, dim), F32), jax.ShapeDtypeStruct((k_rows, dim), F32))
         inside = pl.BlockSpec(memory_space=pltpu.VMEM)
+        operands = (queries.reshape(q_rows, dim), key_vecs.reshape(k_rows, dim), value_vecs.reshape(k_rows, dim), attn_out.reshape(q_rows, dim),
+                    log_sum_exp[0], grad_out.reshape(q_rows, dim))
         results = pl.pallas_call(
             functools.partial(kernel, n, prefix0, dim ** -0.5, n_heads),
             name="exchange_and_backward",
             out_shape=shapes,
-            in_specs=[inside] * 6,
+            in_specs=[anywhere] * 6,
             out_specs=[inside] * 3,
             scratch_shapes=scratch,
             compiler_params=pltpu.CompilerParams(has_side_effects=True, collective_id=0, vmem_limit_bytes=VMEM_MIB * 1024 * 1024),
-        )(queries.reshape(q_rows, dim), key_vecs.reshape(k_rows, dim), value_vecs.reshape(k_rows, dim), attn_out.reshape(q_rows, dim),
-          log_sum_exp[0], grad_out.reshape(q_rows, dim))
+        )(*(pltpu.with_memory_space_constraint(x, pltpu.HBM) for x in operands))
         dq, dk, dv = pl.pallas_call(
             write_out,
             name="write_out",

time: 85.5 us -> 82.8 us (0.968)
  local copies, waits for them, and re-layouts: 5.7 us -> 0 us
  Pallas kernels: 78.9 us -> 82 us
    unnamed x12 -> x0, local copies, waits for them, and re-layouts: 5.7 us -> none
    pallas_call x1, Pallas kernels: 77.2 us -> 80.3 us  [per_device(): pl.pallas_call(functools.partial(kernel, n, prefix0, dim ** (-0.5), n_hea...]
where the time goes in v5:
time: 82.8 us; the launch traced here: 82.6 us
  Pallas kernels  82 us (99%)
    pallas_call x1, Pallas kernels, per_device(): pl.pallas_call(functools.partial(kernel, n, prefix0, dim ** (-0.5), n_hea...  80.3 us

profile of v5, /device:TPU:0, one launch (start us, length us, event | category | flops | bytes accessed | tf_op | source)
XLA Modules:
  0.0 82.6 jit_solution(8879589648418453825)
XLA Ops:
  0.6 80.3 %exchange_and_backward.1 = (bf16[896,128]{1,0:T(8,128)(2,1)S(1)}, f32[2688,128]{1,0:T(8,128)S(1)}, f32[2688,128]{1,0:T(8,128)S(1)}) custom-call(bf16[896,128]{1,0:T(8,128)(2,1)} %bitcast.11, bf16[2688,128]{1,0:T(8,128)(2,1)} %bitcast.9, bf16[2688,128]{1,0:T(8,128)(2,1)} %bitcast.10, bf16[896,128]{1,0:T(8,128)(2,1)} %bitcast.12, f32[16,56]{1,0:T(8,128)} %bitcast.14, ...), custom_call_target="tpu_custom_call" | custom-call | tf_op jit(solution)/shard_map/exchange_and_backward/pallas_call | solution.py:599
  81.0 1.6 %write_out.1 = (bf16[896,128]{1,0:T(8,128)(2,1)}, f32[2688,128]{1,0:T(8,128)}, f32[2688,128]{1,0:T(8,128)}) custom-call(bf16[896,128]{1,0:T(8,128)(2,1)S(1)} %get-tuple-element.9.refs_0_, f32[2688,128]{1,0:T(8,128)S(1)} %get-tuple-element.10.refs_1_, f32[2688,128]{1,0:T(8,128)S(1)} %get-tuple-element.11.refs_2_), custom_call_target="tpu_custom_call" | custom-call | tf_op jit(solution)/shard_map/write_out/pallas_call | solution.py:608
